TPU v7x, 512 devices: a whole 4x8x8 slice. The times are simulated.
512 devices in a mesh: seq: 32 (over x, y), head: 16 (over z, core).
Axes of the slice: x: 4, y: 8, z: 8, core: 2. Of those that a mesh axis runs over, the one named last changes fastest.
Arguments:
- projected: bfloat16 [3, 4096, 2048], P(None, 'seq', 'head'), may hold values from -6 to 6
- out_grad: bfloat16 [4096, 2048], P('seq', 'head'), may hold values from -6 to 6
- logits: float32 [2, 16, 4096], P(None, 'head', 'seq'), may hold values from -6 to 6
- head_params: float32 [2, 16], P(None, 'head'), may hold values from -12 to 1, as said below
- qkv_weight: bfloat16 [3, 2048, 2048], P(None, None, 'head'), may hold values from -0.1875 to 0.1875
- gate_weight: bfloat16 [2, 16, 2048], P(None, 'head'), may hold values from -1.5 to 1.5
Outputs:
- input_grad: bfloat16 [4096, 2048], P('seq', 'head')
Inputs may be any that keep to these rules, and one draw needn't show every extreme that they name: `head_params`: row 0 holds the logarithms of the heads' decay scales, row 1 the decay biases.
All inputs are finite; a program needn't handle non-finite values.
Results may differ from a plain program's by a relative error of at most 0.0034.
Values sent between devices are 32-bit elements; how exact they have to be, the bound alone decides.
No kernel may reach another device: no remote copies, remote signals or barrier semaphores. Data moves between devices by JAX's collectives and lax.ppermute only.
A program may use at most 64 MiB of HBM per device.

v0:
```python
import jax
import jax.numpy as jnp
from jax import lax
from jax.sharding import Mesh
from jax.sharding import PartitionSpec as P

DK = 128
BLOCK = 64
SEQ = ("seq_0", "seq_1")


exact_precision = lax.Precision.HIGHEST


def filled_with(x, identity):
    return jax.tree.map(
        lambda a, e: jnp.broadcast_to(jnp.asarray(e, a.dtype), a.shape), x, identity
    )


def carried_in(x, axes, combine, identity, reverse):
    before = start = filled_with(x, identity)
    running = x
    for axis in reversed(axes):
        peers, here = (lax.axis_size(axis), lax.axis_index(axis))
        pieces = jax.tree.map(lambda part: lax.all_gather(part, axis), running)
        inside, running = (start, start)
        for k in reversed(range(peers)) if reverse else range(peers):
            passed = k > here if reverse else k < here
            running = combine(running, jax.tree.map(lambda part: part[k], pieces))
            inside = jax.tree.map(lambda new, old: jnp.where(passed, new, old), running, inside)
        before = combine(inside, before)
    return before


def cut_along(x, dim, peers):
    shape = x.shape
    pieces = x.reshape(*shape[:dim], peers, shape[dim] // peers, *shape[dim + 1 :])
    return jnp.moveaxis(pieces, dim, 0)


def summed_on_arrival(x, axis, dim):
    pieces = cut_along(x, dim, lax.axis_size(axis))
    arrived = lax.all_to_all(pieces, axis, split_axis=0, concat_axis=0, tiled=True)
    return arrived.sum(axis=0)


def matmul(left, right):
    return jnp.matmul(left, right, precision=exact_precision)


def flip_last(array):
    return jnp.swapaxes(array, -1, -2)


def unit_rows(raw_rows):
    return raw_rows * lax.rsqrt(jnp.sum(raw_rows * raw_rows, axis=-1, keepdims=True) + 1.0)


def to_blocks(array, block_len):
    tok_rows, head_count, depth = array.shape
    return array.reshape(tok_rows // block_len, block_len, head_count, depth).transpose(0, 2, 1, 3)


def prepare(query_raw, key_raw, values, logit_rows, head_params, block_len):
    queries = to_blocks(unit_rows(query_raw) * DK ** (-0.5), block_len)
    keys = to_blocks(unit_rows(key_raw), block_len)
    value_rows = to_blocks(values, block_len)
    decay = -jnp.exp(head_params[0])[:, None] * jax.nn.softplus(
        logit_rows[0] + head_params[1][:, None]
    )
    head_count, tok_rows = decay.shape
    block_count = tok_rows // block_len
    cumul = jnp.cumsum(
        decay.reshape(head_count, block_count, block_len).transpose(1, 0, 2), axis=-1
    )
    write_gate = (
        jax.nn.sigmoid(logit_rows[1]).reshape(head_count, block_count, block_len).transpose(1, 0, 2)
    )
    row_index = lax.broadcasted_iota(jnp.int32, (block_len, block_len), 0)
    col_index = lax.broadcasted_iota(jnp.int32, (block_len, block_len), 1)
    lower_mask = row_index >= col_index
    strict_mask = row_index > col_index
    spread = cumul[..., :, None] - cumul[..., None, :]
    decay_ratio = jnp.where(lower_mask, jnp.exp(jnp.where(lower_mask, spread, 0.0)), 0.0)
    key_inner = matmul(keys, flip_last(keys))
    lower_part = jnp.where(strict_mask, decay_ratio * key_inner * write_gate[..., :, None], 0.0)
    inverse = jnp.eye(block_len, dtype=jnp.float32) - lower_part
    decay_power_matrix = lower_part
    reach_len = 2
    while reach_len < block_len:
        decay_power_matrix = matmul(decay_power_matrix, decay_power_matrix)
        inverse = inverse + matmul(inverse, decay_power_matrix)
        reach_len = reach_len * 2
    decayed = jnp.exp(cumul)
    base_values = matmul(inverse, write_gate[..., None] * value_rows)
    key_weights = matmul(inverse, (write_gate * decayed)[..., None] * keys)
    attend = decay_ratio * matmul(queries, flip_last(keys))
    query_decayed = decayed[..., None] * queries
    key_decayed = jnp.exp(cumul[..., -1:] - cumul)[..., None] * keys
    return (base_values, key_weights, attend, query_decayed, key_decayed, decayed[..., -1])


def block_run(pieces, start_state):

    def block_step(running_state, block_piece):
        base_values, key_weights, attend, query_decayed, key_decayed, last_decay = block_piece
        fresh_values = base_values - matmul(key_weights, running_state)
        out_rows = matmul(query_decayed, running_state) + matmul(attend, fresh_values)
        running_state = last_decay[:, None, None] * running_state + matmul(
            flip_last(key_decayed), fresh_values
        )
        return (running_state, out_rows)

    final_state, out_rows = lax.scan(block_step, start_state, pieces)
    return (out_rows, final_state)


def transition(pieces, eye_state):
    base_values, key_weights, attend, query_decayed, key_decayed, last_decay = pieces
    block_maps = last_decay[..., None, None] * eye_state - matmul(
        flip_last(key_decayed), key_weights
    )
    block_start_positions = matmul(flip_last(key_decayed), base_values)

    def transition_step(carry_pair, block_pair):
        step_matrix, offset = carry_pair
        block_map, block_offset = block_pair
        return ((matmul(block_map, step_matrix), matmul(block_map, offset) + block_offset), None)

    start_pair = (eye_state, jnp.zeros_like(eye_state))
    final_pair, unused = lax.scan(transition_step, start_pair, (block_maps, block_start_positions))
    return final_pair


def compose(earlier, later):
    return (matmul(later[0], earlier[0]), matmul(later[0], earlier[1]) + later[1])


def shards(projected, out_grad, logits, head_params, qkv_weight, gate_weight):
    tok_rows = projected.shape[1]
    head_count = projected.shape[2] // DK
    raw_inputs = projected.astype(jnp.float32).reshape(3, tok_rows, head_count, DK)
    out_blocks = to_blocks(out_grad.astype(jnp.float32).reshape(tok_rows, head_count, DK), BLOCK)

    def prep_fn(query_raw, key_raw, values, logit_rows):
        return prepare(query_raw, key_raw, values, logit_rows, head_params, BLOCK)

    pieces, pull_prepare = jax.vjp(prep_fn, raw_inputs[0], raw_inputs[1], raw_inputs[2], logits)
    eye_state = jnp.broadcast_to(jnp.eye(DK, dtype=jnp.float32), (head_count, DK, DK))
    zero_state = jnp.zeros((head_count, DK, DK), jnp.float32)
    step_matrix, offset = transition(pieces, eye_state)

    def state_only(start_state):
        return block_run(pieces, start_state)

    unused_out, pull_state = jax.vjp(state_only, zero_state)
    free_grad = pull_state((out_blocks, zero_state))[0]
    state_in = carried_in((step_matrix, offset), SEQ, compose, (eye_state, zero_state), False)[1]
    grad_out = carried_in(
        (flip_last(step_matrix), free_grad), SEQ, compose, (eye_state, zero_state), True
    )[1]
    unused_run, pull_run = jax.vjp(block_run, pieces, state_in)
    piece_grads, unused_grad = pull_run((out_blocks, grad_out))
    query_grad, key_grad, value_grad, logit_grad = pull_prepare(piece_grads)
    stacked_gradient = (
        jnp.stack([query_grad, key_grad, value_grad])
        .reshape(3, tok_rows, head_count * DK)
        .astype(jnp.bfloat16)
    )
    partial_term = jnp.einsum(
        "jtk,jdk->td", stacked_gradient, qkv_weight, preferred_element_type=jnp.float32
    )
    partial_term = partial_term + jnp.einsum(
        "jht,jhd->td", logit_grad, gate_weight.astype(jnp.float32), precision=exact_precision
    )
    return summed_on_arrival(partial_term, "head", 1).astype(jnp.bfloat16)


def solution(mesh):
    split = Mesh(mesh.devices.reshape(4, 8, mesh.shape["head"]), ("seq_0", "seq_1", "head"))
    in_specs = (
        P(None, SEQ, "head"),
        P(SEQ, "head"),
        P(None, "head", SEQ),
        P(None, "head"),
        P(None, None, "head"),
        P(None, "head", None),
    )
    out_specs = P(SEQ, "head")
    return jax.shard_map(
        shards, mesh=split, in_specs=in_specs, out_specs=out_specs, check_vma=False
    )
```

profile of v0, /device:TPU:1, one launch (start us, length us, event | category | flops | bytes accessed | tf_op | source)
XLA Modules:
  0.0 267.7 jit_solution(604900775022704233)
XLA Ops:
  1.9 1.3 fusion.314
  3.8 2.5 fusion.310
  16.2 21.8 %all-gather.4 = f32[8,128,128]{2,1,0:T(8,128)S(1)} all-gather(f32[1,128,128]{2,1,0:T(8,128)S(1)} %get-tuple-element.769), channel_id=6, replica_groups=mesh['seq_0'=4,'seq_1'=8,'head'=16] {'seq_1'}, dimensions={0}, use_global_device_ids=true | all-gather | bytes 589824 | tf_op jit(solution)/shard_map/all_gather | solution.py:26
  38.6 19.8 %all-gather.6 = f32[8,128,128]{2,1,0:T(8,128)S(1)} all-gather(f32[1,128,128]{2,1,0:T(8,128)S(1)} %get-tuple-element.776), channel_id=8, replica_groups=mesh['seq_0'=4,'seq_1'=8,'head'=16] {'seq_1'}, dimensions={0}, use_global_device_ids=true | all-gather | bytes 589824 | tf_op jit(solution)/shard_map/all_gather | solution.py:26
  60.3 9.7 %all-gather.7 = f32[512,128]{1,0:T(8,128)S(1)} all-gather(f32[128,128]{1,0:T(8,128)S(1)} %convolution_add_fusion.28), channel_id=9, replica_groups=mesh['seq_0'=4,'seq_1'=8,'head'=16] {'seq_0'}, dimensions={0}, use_global_device_ids=true | all-gather | bytes 327680 | tf_op jit(solution)/shard_map/all_gather | solution.py:26
  71.6 9.4 %all-gather.5 = f32[512,128]{1,0:T(8,128)S(1)} all-gather(f32[128,128]{1,0:T(8,128)S(1)} %fusion.187), channel_id=7, replica_groups=mesh['seq_0'=4,'seq_1'=8,'head'=16] {'seq_0'}, dimensions={0}, use_global_device_ids=true | all-gather | bytes 327680 | tf_op jit(solution)/shard_map/all_gather | solution.py:26
  84.9 8.6 %while.103 = (s32[]{:T(128)}, f32[1,128,128]{2,1,0:T(8,128)S(1)}, f32[2,128,128]{2,1,0:T(8,128)S(1)}, f32[2,64,128]{2,1,0:T(8,128)}, f32[2,64,128]{2,1,0:T(8,128...) while((s32[]{:T(128)}, f32[1,128,128]{2,1,0:T(8,128)S(1)}, ...), condition=%wide.region_10.11_spmd, body=%wide.region_9.10_spmd.sunk | while | flops 25206784 | bytes 1018065 | solution.py:115
  85.7 1.2 constant_dynamic-slice_fusion.9
  90.0 1.2 constant_dynamic-slice_fusion.9
  93.6 4.0 %while.102 = (s32[]{:T(128)}, f32[2,64,128]{2,1,0:T(8,128)S(1)}, f32[2,64,128]{2,1,0:T(8,128)S(1)}, f32[2,64,64]{2,1,0:T(8,128)S(1)}, f32[2,1,1,1]{0,3,2,1:T(1,1...) while((s32[]{:T(128)}, f32[2,64,128]{2,1,0:T(8,128)S(1)}, ...), condition=%wide.region_6.7_spmd, body=%wide.region_5.6_spmd.sunk | while | flops 2 | bytes 327841 | solution.py:115
  93.6 1.2 constant_dynamic-slice_fusion.8
  95.6 1.2 constant_dynamic-slice_fusion.8
  97.6 4.9 %while.105 = (s32[]{:T(128)}, f32[1,128,128]{2,1,0:T(8,128)S(1)}, f32[2,1,1,1]{0,3,2,1:T(1,128)S(1)}, f32[2,64,128]{2,1,0:T(8,128)S(1)}, f32[2,1,64,128]{3,2,1,0...) while((s32[]{:T(128)}, f32[1,128,128]{2,1,0:T(8,128)S(1)}, ...), condition=%wide.region_8.9_spmd.clone, body=%wide.region_7.8_spmd.clone.sunk | while | flops 44138500 | bytes 690835 | solution.py:115
  102.5 19.5 %all-gather.2 = f32[8,128,128]{2,1,0:T(8,128)S(1)} all-gather(f32[1,128,128]{2,1,0:T(8,128)S(1)} %get-tuple-element.775), channel_id=4, replica_groups=mesh['seq_0'=4,'seq_1'=8,'head'=16] {'seq_1'}, dimensions={0}, use_global_device_ids=true | all-gather | bytes 589824 | tf_op jit(solution)/shard_map/all_gather | solution.py:26
  122.1 20.4 %all-gather = f32[8,128,128]{2,1,0:T(8,128)S(1)} all-gather(f32[1,128,128]{2,1,0:T(8,128)S(1)} %bitcast.764), channel_id=2, replica_groups=mesh['seq_0'=4,'seq_1'=8,'head'=16] {'seq_1'}, dimensions={0}, use_global_device_ids=true | all-gather | bytes 589824 | tf_op jit(solution)/shard_map/all_gather | solution.py:26
  144.3 9.7 %all-gather.3 = f32[512,128]{1,0:T(8,128)S(1)} all-gather(f32[128,128]{1,0:T(8,128)S(1)} %convolution_add_fusion.41), channel_id=5, replica_groups=mesh['seq_0'=4,'seq_1'=8,'head'=16] {'seq_0'}, dimensions={0}, use_global_device_ids=true | all-gather | bytes 327680 | tf_op jit(solution)/shard_map/all_gather | solution.py:26
  155.5 9.8 %all-gather.1 = f32[512,128]{1,0:T(8,128)S(1)} all-gather(f32[128,128]{1,0:T(8,128)S(1)} %fusion.180), channel_id=3, replica_groups=mesh['seq_0'=4,'seq_1'=8,'head'=16] {'seq_0'}, dimensions={0}, use_global_device_ids=true | all-gather | bytes 327680 | tf_op jit(solution)/shard_map/all_gather | solution.py:26
  166.8 14.5 %while.104 = (s32[]{:T(128)}, f32[1,128,128]{2,1,0:T(8,128)S(1)}, f32[2,1,64,128]{3,2,1,0:T(8,128)S(1)}, f32[2,1,64,128]{3,2,1,0:T(8,128)S(1)}, f32[2,1,64,64]{2...) while((s32[]{:T(128)}, f32[1,128,128]{2,1,0:T(8,128)S(1)}, ...), condition=%wide.region_13.14_spmd, body=%wide.region_11.13_spmd.sunk | while | flops 88186880 | bytes 1351905 | solution.py:115
  167.4 1.0 convolution_bitcast_fusion.20
  168.7 1.5 fusion.496
  170.9 1.7 fusion.491
  175.9 1.5 fusion.496
  178.1 1.7 fusion.491
  193.9 73.1 %all_to_all.5 = f32[16,128,128]{2,1,0:T(8,128)S(1)} all-to-all(f32[16,128,128]{2,1,0:T(8,128)S(1)} %bitcast.743), channel_id=1, replica_groups=mesh['seq_0'=4,'seq_1'=8,'head'=16] {'head'}, dimensions={0} | all-to-all | bytes 2097152 | tf_op jit(solution)/shard_map/all_to_all | solution.py:44
  (308 shorter events, 56.4 us)
Async XLA Ops:
  0.0 192.5 %copy-start = (bf16[3,2048,128]{2,1,0:T(8,128)(2,1)S(1)}, bf16[3,2048,128]{2,1,0:T(8,128)(2,1)}, u32[]{:S(2)}) copy-start(bf16[3,2048,128]{2,1,0:T(8,128)(2,1)} %param.20) | copy-start | bytes 4718596
  1.8 11.5 %copy-start.1 = (f32[1,128,128]{2,1,0:T(8,128)}, f32[1,128,128]{2,1,0:T(8,128)S(1)}, u32[]{:S(2)}) copy-start(f32[1,128,128]{2,1,0:T(8,128)S(1)} %get-tuple-element.1098) | copy-start | bytes 196612
  1.9 7.2 %copy-start.17 = (pred[64,64]{0,1:T(8,128)(4,1)}, pred[64,64]{0,1:T(8,128)(4,1)S(1)}, u32[]{:S(2)}) copy-start(pred[64,64]{0,1:T(8,128)(4,1)S(1)} %iota_compare_fusion.9) | copy-start | bytes 12292
  1.9 7.2 %copy-start.15 = (f32[64,64]{0,1:T(8,128)}, f32[64,64]{0,1:T(8,128)S(1)}, u32[]{:S(2)}) copy-start(f32[64,64]{0,1:T(8,128)S(1)} %fusion.252) | copy-start | bytes 49156
  7.8 4.4 %copy-start.38 = (f32[2]{0:T(128)}, f32[2]{0:T(128)S(1)}, u32[]{:S(2)}) copy-start(f32[2]{0:T(128)S(1)} %slice_reduce_fusion) | copy-start | bytes 28
  8.0 4.0 %copy-start.33 = (f32[128]{0:T(128)}, f32[128]{0:T(128)S(1)}, u32[]{:S(2)}) copy-start(f32[128]{0:T(128)S(1)} %get-tuple-element.967) | copy-start | bytes 1540
  8.2 5.6 %copy-start.20 = (f32[2,64]{1,0:T(2,128)}, f32[2,64]{1,0:T(2,128)S(1)}, u32[]{:S(2)}) copy-start(f32[2,64]{1,0:T(2,128)S(1)} %div.45) | copy-start | bytes 1540
  71.3 11.1 %copy-start.24 = (f32[2,64]{1,0:T(2,128)S(1)}, f32[2,64]{1,0:T(2,128)}, u32[]{:S(2)}) copy-start(f32[2,64]{1,0:T(2,128)} %copy-done.23) | copy-start | bytes 1540
  93.5 4.1 %copy-start.22 = (bf16[128,128]{1,0:T(8,128)(2,1)S(1)}, bf16[128,128]{1,0:T(8,128)(2,1)}, u32[]{:S(2)}) copy-start(bf16[128,128]{1,0:T(8,128)(2,1)} %param.17) | copy-start | bytes 98308
  97.6 24.5 %copy-start.19 = (f32[1,128,128]{1,2,0:T(8,128)S(1)}, f32[1,128,128]{1,2,0:T(8,128)}, u32[]{:S(2)}) copy-start(f32[1,128,128]{1,2,0:T(8,128)} %copy.174) | copy-start | bytes 196612
  166.8 14.8 %copy-start.27 = (f32[2,64]{1,0:T(2,128)S(1)}, f32[2,64]{1,0:T(2,128)}, u32[]{:S(2)}) copy-start(f32[2,64]{1,0:T(2,128)} %copy-done.26) | copy-start | bytes 1540
  166.8 15.1 %copy-start.2 = (f32[1,128,128]{2,1,0:T(8,128)S(1)}, f32[1,128,128]{2,1,0:T(8,128)}, u32[]{:S(2)}) copy-start(f32[1,128,128]{2,1,0:T(8,128)} %copy-done.1) | copy-start | bytes 196612
  166.8 15.1 %copy-start.21 = (f32[2,64]{1,0:T(2,128)S(1)}, f32[2,64]{1,0:T(2,128)}, u32[]{:S(2)}) copy-start(f32[2,64]{1,0:T(2,128)} %copy-done.20) | copy-start | bytes 1540
  166.8 15.4 %copy-start.6 = (f32[2,64,64]{2,1,0:T(8,128)S(1)}, f32[2,64,64]{2,1,0:T(8,128)}, u32[]{:S(2)}) copy-start(f32[2,64,64]{2,1,0:T(8,128)} %copy-done.5) | copy-start | bytes 98308
  166.8 15.6 %copy-start.4 = (f32[2,64,64]{1,2,0:T(8,128)S(1)}, f32[2,64,64]{1,2,0:T(8,128)}, u32[]{:S(2)}) copy-start(f32[2,64,64]{1,2,0:T(8,128)} %copy-done.3) | copy-start | bytes 98308
  181.3 3.6 %copy-start.8 = (f32[2,64,64]{1,2,0:T(8,128)S(1)}, f32[2,64,64]{1,2,0:T(8,128)}, u32[]{:S(2)}) copy-start(f32[2,64,64]{1,2,0:T(8,128)} %copy-done.7) | copy-start | bytes 98308
  183.9 3.7 %copy-start.14 = (f32[2,64,64]{1,2,0:T(8,128)S(1)}, f32[2,64,64]{1,2,0:T(8,128)}, u32[]{:S(2)}) copy-start(f32[2,64,64]{1,2,0:T(8,128)} %copy-done.13) | copy-start | bytes 98308
  185.5 3.8 %copy-start.37 = (f32[1,1,128]{2,1,0:T(1,128)S(1)}, f32[1,1,128]{2,1,0:T(1,128)}, u32[]{:S(2)}) copy-start(f32[1,1,128]{2,1,0:T(1,128)} %get-tuple-element.1086) | copy-start | bytes 1540
  185.5 3.9 %copy-start.39 = (f32[2]{0:T(128)S(1)}, f32[2]{0:T(128)}, u32[]{:S(2)}) copy-start(f32[2]{0:T(128)} %copy-done.38) | copy-start | bytes 28
  185.5 5.2 %copy-start.32 = (f32[2,1,128]{2,1,0:T(1,128)S(1)}, f32[2,1,128]{2,1,0:T(1,128)}, u32[]{:S(2)}) copy-start(f32[2,1,128]{2,1,0:T(1,128)} %param.18) | copy-start | bytes 3076
  185.6 5.9 %copy-start.31 = (f32[2,64]{1,0:T(2,128)S(1)}, f32[2,64]{1,0:T(2,128)}, u32[]{:S(2)}) copy-start(f32[2,64]{1,0:T(2,128)} %get-tuple-element.1104) | copy-start | bytes 1540
  186.6 5.6 %copy-start.34 = (f32[128]{0:T(128)S(1)}, f32[128]{0:T(128)}, u32[]{:S(2)}) copy-start(f32[128]{0:T(128)} %copy-done.33) | copy-start | bytes 1540
  186.6 5.6 %copy-start.36 = (f32[128]{0:T(128)S(1)}, f32[128]{0:T(128)}, u32[]{:S(2)}) copy-start(f32[128]{0:T(128)} %copy-done.35) | copy-start | bytes 1540
  186.6 5.6 %copy-start.41 = (f32[128]{0:T(128)S(1)}, f32[128]{0:T(128)}, u32[]{:S(2)}) copy-start(f32[128]{0:T(128)} %copy-done.40) | copy-start | bytes 1540
  (18 other events, 40.4 us)
where the time goes:
time: 269 us; the launch traced here: 268 us
  blocking collectives  193 us (72%)
  matrix products  37.6 us (14%)
  local copies, waits for them, and re-layouts  23.1 us (9%)
  other arithmetic  11.1 us (4%)
    all_gather x8, blocking collectives, carried_in(): pieces = jax.tree.map(lambda part: lax.all_gather(part, axis), running)  120 us
    all_to_all x1, blocking collectives, summed_on_arrival(): lax.all_to_all(pieces, axis, split_axis=0, concat_axis=0, tiled=True)  73.1 us
    dot_general x122, matrix products, matmul(): return jnp.matmul(left, right, precision=exact_precision)  36.3 us
    dynamic_slice x8, local copies, waits for them, and re-layouts, block_run(): final_state, out_rows = lax.scan(block_step, start_state, pieces)  7.53 us
    dynamic_update_slice x22, local copies, waits for them, and re-layouts, block_run(): final_state, out_rows = lax.scan(block_step, start_state, pieces)  6.96 us

commit v1 on v0

v1 whole, which is shorter than its diff:
```python
import jax
import jax.numpy as jnp
from jax import lax
from jax.experimental import pallas as pl
from jax.experimental.pallas import tpu as pltpu
from jax.sharding import Mesh
from jax.sharding import PartitionSpec as P

DK = 128
TOK = 128
ROWS = 4
COLS = 8
SLICE = DK // COLS
SCALE = DK ** (-0.5)
F32 = jnp.float32

NN = (((1,), (0,)), ((), ()))
NT = (((1,), (1,)), ((), ()))
TN = (((0,), (0,)), ((), ()))


BF16 = jnp.bfloat16


def halves(x):
    if isinstance(x, tuple):
        return x
    high = x.astype(BF16)
    return high, (x - high.astype(F32)).astype(BF16)


def dot(left, right, dims=NN):
    (lh, ll), (rh, rl) = halves(left), halves(right)

    def one(a, b):
        return lax.dot_general(a, b, dims, preferred_element_type=F32)

    return one(lh, rh) + (one(lh, rl) + one(ll, rh))


def iotas():
    row = lax.broadcasted_iota(jnp.int32, (TOK, TOK), 0)
    col = lax.broadcasted_iota(jnp.int32, (TOK, TOK), 1)
    return row, col


def lane_sum(x):
    return jnp.sum(x, axis=1, keepdims=True)


def unit(raw):
    scale = lax.rsqrt(lane_sum(raw * raw) + 1.0)
    return raw * scale, scale


def gates(logit_ref, head_ref, row, col):
    rate = jnp.exp(jnp.full((1, TOK), head_ref[0, 0], F32))
    shifted = logit_ref[0] + head_ref[1, 0]
    soft = jnp.maximum(shifted, 0.0) + jnp.log1p(jnp.exp(-jnp.abs(shifted)))
    decay_row = -rate * soft
    cumul = lane_sum(jnp.where(col <= row, decay_row, 0.0))
    cumul_row = jnp.sum(jnp.where(row == col, cumul, 0.0), axis=0, keepdims=True)
    last = cumul_row[:, TOK - 1 :]
    write = lane_sum(jnp.where(row == col, jax.nn.sigmoid(logit_ref[1]), 0.0))
    lower = row >= col
    ratio = jnp.where(lower, jnp.exp(jnp.where(lower, cumul - cumul_row, 0.0)), 0.0)
    slope = lane_sum(jnp.where(row == col, -rate * jax.nn.sigmoid(shifted), 0.0))
    return jnp.exp(cumul), jnp.exp(last - cumul), jnp.exp(last), write, ratio, slope


def inverse_of(strict, row, col):
    eye = jnp.where(row == col, 1.0, 0.0).astype(F32)
    near = jnp.where((row >> 3) == (col >> 3), strict, 0.0)
    power2 = dot(near, near)
    out = eye - near
    both = dot(jnp.concatenate([out, power2], 0), power2)
    out, power4 = out + both[:TOK], both[TOK:]
    out = out + dot(out, power4)
    for level in (3, 4, 5, 6):
        joined = ((row >> (level + 1)) == (col >> (level + 1))) & ((row >> level) != (col >> level))
        off = jnp.where(joined, strict, 0.0)
        pair = halves(out)
        out = out - dot(pair, dot(off, pair))
    return out


def chunk_kernel(proj_ref, grad_ref, logit_ref, head_ref, out_ref, saved_ref):
    row, col = iotas()
    grown, rest, total, write, ratio, _ = gates(logit_ref, head_ref, row, col)
    queries = unit(proj_ref[0].astype(F32))[0] * SCALE
    keys = unit(proj_ref[1].astype(F32))[0]
    values = proj_ref[2].astype(F32)
    out_grad = grad_ref[...].astype(F32)
    inner = dot(jnp.concatenate([keys, queries], 0), keys, NT)
    bare = jnp.where(row > col, ratio * inner[:TOK], 0.0)
    attend = ratio * inner[TOK:]
    inverse = inverse_of(bare * write, row, col)
    solved = dot(inverse, jnp.concatenate([(write * grown) * keys, write * values], 1))
    key_weights, base = solved[:, :DK], solved[:, DK:]
    rest_keys = rest * keys
    moved = dot(solved, rest_keys, TN)
    eye = jnp.where(row == col, 1.0, 0.0).astype(F32)
    step = total * eye - moved[:DK]
    offset = moved[DK:]
    back = dot(out_grad, grown * queries - dot(attend, key_weights), TN)
    for peer in range(COLS):
        out_ref[peer, :DK] = step
        out_ref[peer, DK : DK + SLICE] = offset[peer * SLICE : (peer + 1) * SLICE]
        out_ref[peer, DK + SLICE :] = back[peer * SLICE : (peer + 1) * SLICE]
    saved_ref[0] = inverse.T
    saved_ref[1] = key_weights
    saved_ref[2] = base
    saved_ref[3] = attend
    saved_ref[4] = bare
    saved_ref[5] = dot(attend, out_grad, TN)


def row_kernel(in_ref, out_ref, own_ref, scratch_ref):
    here_x = lax.axis_index("x")
    here_y = lax.axis_index("y")
    step = [in_ref[j, :DK] for j in range(COLS)]
    ahead = [in_ref[j, DK : DK + SLICE] for j in range(COLS)]
    back = [in_ref[j, DK + SLICE :] for j in range(COLS)]

    def joined(first, second):
        both = dot(jnp.concatenate([first[0], first[1]], 0), second[0])
        return (both[:DK], both[DK:] + second[1], first[2] + dot(second[2], first[0], NT))

    ones = list(zip(step, ahead, back))
    pairs = [joined(ones[2 * i], ones[2 * i + 1]) for i in range(4)]
    quads = [joined(pairs[2 * i], pairs[2 * i + 1]) for i in range(2)]
    whole = joined(quads[0], quads[1])

    zero = jnp.zeros((SLICE, DK), F32)
    b4 = quads[0][1]
    b2 = pairs[0][1]
    b6 = dot(b4, pairs[2][0]) + pairs[2][1]
    prefix = [
        zero,
        ahead[0],
        b2,
        dot(b2, step[2]) + ahead[2],
        b4,
        dot(b4, step[4]) + ahead[4],
        b6,
        dot(b6, step[6]) + ahead[6],
    ]
    c3 = quads[1][2]
    c5 = pairs[3][2]
    c1 = dot(c3, pairs[1][0], NT) + pairs[1][2]
    suffix = [
        dot(c1, step[1], NT) + back[1],
        c1,
        dot(c3, step[3], NT) + back[3],
        c3,
        dot(c5, step[5], NT) + back[5],
        c5,
        back[7],
        zero,
    ]

    row, col = iotas()
    eye = jnp.where(row == col, 1.0, 0.0).astype(F32)
    at_y = jnp.full((DK, DK), here_y, jnp.int32)
    high = at_y >= 4
    mid = (at_y & 2) != 0
    low = (at_y & 1) != 0
    before = jnp.where(high, quads[0][0], eye)
    before = dot(before, jnp.where(mid, jnp.where(high, pairs[2][0], pairs[0][0]), eye))
    single = in_ref[jnp.maximum(here_y - 1, 0), :DK]
    own_ref[0] = dot(before, jnp.where(low, single, eye))
    after = jnp.where(high, eye, quads[1][0])
    after = dot(jnp.where(mid, eye, jnp.where(high, pairs[3][0], pairs[1][0])), after)
    single = in_ref[jnp.minimum(here_y + 1, COLS - 1), :DK]
    own_ref[1] = dot(jnp.where(low, eye, single), after)

    scratch_ref[...] = whole[0]
    piece = scratch_ref[pl.ds(pl.multiple_of(here_y * SLICE, SLICE), SLICE)]
    for peer_x in range(ROWS):
        own = jnp.full((SLICE, DK), here_x, jnp.int32) == peer_x
        for peer_y in range(COLS):
            slot = peer_x * COLS + peer_y
            out_ref[slot, :SLICE] = piece
            out_ref[slot, SLICE : 2 * SLICE] = jnp.where(own, prefix[peer_y], whole[1])
            out_ref[slot, 2 * SLICE :] = jnp.where(own, suffix[peer_y], whole[2])


def grad_kernel(
    proj_ref,
    grad_ref,
    logit_ref,
    head_ref,
    weight_hbm,
    gate_ref,
    saved_ref,
    own_ref,
    in_ref,
    keep_ref,
    send_ref,
    weight_ref,
    sem,
):
    fetch = pltpu.make_async_copy(weight_hbm, weight_ref, sem)
    fetch.start()
    here_x = lax.axis_index("x")
    here_c = lax.axis_index("c")

    def part(row_at, kind):
        rows = pl.ds(row_at * COLS, COLS)
        return in_ref[rows, kind * SLICE : (kind + 1) * SLICE].reshape(DK, DK)

    step1, step2 = part(1, 0), part(2, 0)
    s1 = part(0, 1)
    s2 = dot(s1, step1) + part(1, 1)
    s3 = dot(s2, step2) + part(2, 1)
    g2 = part(3, 2)
    g1 = dot(g2, step2, NT) + part(2, 2)
    g0 = dot(g1, step1, NT) + part(1, 2)
    zero = jnp.zeros((DK, DK), F32)
    s_row = jnp.where(here_x == 0, zero, jnp.where(here_x == 1, s1, jnp.where(here_x == 2, s2, s3)))
    g_row = jnp.where(here_x == 3, zero, jnp.where(here_x == 2, g2, jnp.where(here_x == 1, g1, g0)))
    state = dot(s_row, own_ref[0]) + part(here_x, 1)
    later = dot(g_row, own_ref[1], NT) + part(here_x, 2)

    row, col = iotas()
    grown, rest, total, write, ratio, slope = gates(logit_ref, head_ref, row, col)
    q_unit, q_scale = unit(proj_ref[0].astype(F32))
    queries = q_unit * SCALE
    keys, k_scale = unit(proj_ref[1].astype(F32))
    values = proj_ref[2].astype(F32)
    out_grad = grad_ref[...].astype(F32)
    rest_keys = rest * keys
    attend = saved_ref[3]
    bare = saved_ref[4]

    fresh = saved_ref[2] - dot(saved_ref[1], state, NT)
    d_fresh = saved_ref[5] + dot(rest_keys, later, NT)
    pulled = dot(saved_ref[0], d_fresh)
    both = dot(jnp.concatenate([out_grad, pulled], 0), state)
    d_query_decayed = both[:TOK]
    d_weighted = -both[TOK:]
    d_rest = dot(fresh, later)
    both = dot(jnp.concatenate([out_grad, pulled], 0), fresh, NT)
    d_attend = jnp.where(row >= col, both[:TOK], 0.0)
    d_lower = jnp.where(row > col, -both[TOK:], 0.0)
    d_qk = d_attend * ratio
    d_kk = d_lower * ratio * write
    stacked = jnp.concatenate([d_qk, d_kk], 0)
    by_key = dot(stacked, keys)
    across = dot(stacked, jnp.concatenate([queries, keys], 0), TN)
    d_queries = grown * d_query_decayed + by_key[:TOK]
    d_keys = by_key[TOK:] + across + rest * d_rest + (write * grown) * d_weighted

    lower_hit = d_lower * bare
    ratio_hit = d_attend * attend + lower_hit * write
    weighted_hit = grown * lane_sum(d_weighted * keys)
    rest_hit = lane_sum(d_rest * rest_keys)
    d_write = lane_sum(pulled * values) + weighted_hit + lane_sum(lower_hit)
    d_cumul = (
        lane_sum(ratio_hit)
        + grown * lane_sum(d_query_decayed * queries)
        - rest_hit
        + write * weighted_hit
    )
    d_cumul_row = jnp.sum(jnp.where(row == col, d_cumul, 0.0) - ratio_hit, axis=0, keepdims=True)
    at_end = jnp.sum(rest_hit, axis=0, keepdims=True) + total * jnp.sum(
        lane_sum(later * state), axis=0, keepdims=True
    )
    d_decay = lane_sum(jnp.where(col >= row, d_cumul_row, 0.0)) + at_end
    d_logit0 = d_decay * slope
    d_logit1 = d_write * write * (1.0 - write)

    d_queries = d_queries * SCALE
    grad_q = q_scale * (d_queries - q_unit * lane_sum(q_unit * d_queries))
    grad_k = k_scale * (d_keys - keys * lane_sum(keys * d_keys))
    grad_v = write * pulled
    low_qk = jnp.concatenate([grad_q, grad_k], 1).astype(jnp.bfloat16)
    low_v = grad_v.astype(jnp.bfloat16)

    fetch.wait()
    for peer in range(COLS):
        rows = pl.ds(peer * 2 * DK, 2 * DK)
        weights = jnp.concatenate([weight_ref[0, rows], weight_ref[1, rows]], 1)
        acc = lax.dot_general(low_qk, weights, NT, preferred_element_type=F32)
        acc = acc + lax.dot_general(low_v, weight_ref[2, rows], NT, preferred_element_type=F32)
        acc = acc + d_logit0 * gate_ref[0, :, rows].astype(F32)
        acc = acc + d_logit1 * gate_ref[1, :, rows].astype(F32)
        keep_ref[peer] = jnp.where(here_c == 0, acc[:, :DK], acc[:, DK:])
        send_ref[peer] = jnp.where(here_c == 0, acc[:, DK:], acc[:, :DK])


VMEM = pl.BlockSpec(memory_space=pltpu.VMEM)
SMEM = pl.BlockSpec(memory_space=pltpu.SMEM)
ANY = pl.BlockSpec(memory_space=pl.ANY)


def like(*shape):
    return jax.ShapeDtypeStruct(shape, F32)


def shards(projected, out_grad, logits, head_params, qkv_weight, gate_weight):
    chunks, saved = pl.pallas_call(
        chunk_kernel,
        out_shape=(like(COLS, DK + 2 * SLICE, DK), like(6, DK, DK)),
        in_specs=[VMEM, VMEM, VMEM, SMEM],
        out_specs=(VMEM, VMEM),
        name="chunk",
    )(projected, out_grad, logits, head_params)
    chunks = lax.all_to_all(chunks, "y", 0, 0, tiled=True)
    rows, own = pl.pallas_call(
        row_kernel,
        out_shape=(like(ROWS * COLS, 3 * SLICE, DK), like(2, DK, DK)),
        in_specs=[VMEM],
        out_specs=(VMEM, VMEM),
        scratch_shapes=[pltpu.VMEM((DK, DK), F32)],
        name="row",
    )(chunks)
    rows = lax.all_to_all(rows, ("x", "y"), 0, 0, tiled=True)
    keep, send = pl.pallas_call(
        grad_kernel,
        out_shape=(like(COLS, TOK, DK), like(COLS, TOK, DK)),
        in_specs=[VMEM, VMEM, VMEM, SMEM, ANY, VMEM, VMEM, VMEM, VMEM],
        out_specs=(VMEM, VMEM),
        scratch_shapes=[
            pltpu.VMEM((3, 2048, DK), jnp.bfloat16),
            pltpu.SemaphoreType.DMA(()),
        ],
        name="grad",
    )(projected, out_grad, logits, head_params, qkv_weight, gate_weight, saved, own, rows)
    other = lax.ppermute(send, "c", [(0, 1), (1, 0)])
    summed = lax.all_to_all(keep + other, "z", 0, 0, tiled=True)
    return summed.sum(axis=0).astype(jnp.bfloat16)


def solution(mesh):
    split = Mesh(mesh.devices.reshape(4, 8, 8, 2), ("x", "y", "z", "c"))
    seq, head = ("x", "y"), ("z", "c")
    in_specs = (
        P(None, seq, head),
        P(seq, head),
        P(None, head, seq),
        P(None, head),
        P(None, None, head),
        P(None, head, None),
    )
    return jax.shard_map(
        shards, mesh=split, in_specs=in_specs, out_specs=P(seq, head), check_vma=False
    )
```

time: 269 us -> 105 us (0.39)
  blocking collectives: 193 us -> 51.2 us
  matrix products: 37.6 us -> 0 us
  waiting for transfers between devices: 0 us -> 20.8 us
  local copies, waits for them, and re-layouts: 23.1 us -> 2.83 us
  starting transfers between devices: 0 us -> 14.4 us
  Pallas kernels: 0 us -> 13 us
  other arithmetic: 11.1 us -> 1.77 us
    all_gather x8 -> x0, blocking collectives: 120 us -> none  [carried_in(): pieces = jax.tree.map(lambda part: lax.all_gather(part, axis), running)]
    dot_general x124 -> x0, matrix products: 37.6 us -> none  [the longest x122 36.3 us: matmul(): return jnp.matmul(left, right, precision=exact_precision)]
    all_to_all x1 -> x2, blocking collectives: 73.1 us -> 51.2 us  [the longest x1 26.6 us: shards(): summed = lax.all_to_all(keep + other, 'z', 0, 0, tiled=True)]
    all_to_all x0 -> x1, waiting for transfers between devices: none -> 19.1 us  [shards(): rows = lax.all_to_all(rows, ('x', 'y'), 0, 0, tiled=True)]
    pallas_call x0 -> x3, Pallas kernels: none -> 13 us  [the longest x1 4.78 us: shards(): pl.pallas_call(grad_kernel, out_shape=(like(COLS, TOK, DK), like(COLS, TO...]
    all_to_all x0 -> x1, starting transfers between devices: none -> 7.89 us  [shards(): rows = lax.all_to_all(rows, ('x', 'y'), 0, 0, tiled=True)]
    dynamic_slice x8 -> x0, local copies, waits for them, and re-layouts: 7.53 us -> none  [block_run(): final_state, out_rows = lax.scan(block_step, start_state, pieces)]
    dynamic_update_slice x22 -> x0, local copies, waits for them, and re-layouts: 6.96 us -> none  [block_run(): final_state, out_rows = lax.scan(block_step, start_state, pieces)]
  transfers between devices with their start and end apart: 0 -> 2, of which waited for: 0 -> 2; matrix products, arithmetic and copies ran while one was open for 0% -> 1% of each run, Pallas kernels for 0% -> 0%
where the time goes in v1:
time: 105 us; the launch traced here: 104 us
  blocking collectives  51.2 us (49%)
  waiting for transfers between devices  20.8 us (20%)
  starting transfers between devices  14.4 us (14%)
  Pallas kernels  13 us (12%)
  local copies, waits for them, and re-layouts  2.83 us (3%)
  other arithmetic  1.77 us (2%)
    all_to_all x1, blocking collectives, shards(): summed = lax.all_to_all(keep + other, 'z', 0, 0, tiled=True)  26.6 us
    all_to_all x1, blocking collectives, shards(): chunks = lax.all_to_all(chunks, 'y', 0, 0, tiled=True)  24.6 us
    all_to_all x1, waiting for transfers between devices, shards(): rows = lax.all_to_all(rows, ('x', 'y'), 0, 0, tiled=True)  19.1 us
    all_to_all x1, starting transfers between devices, shards(): rows = lax.all_to_all(rows, ('x', 'y'), 0, 0, tiled=True)  7.89 us
    ppermute x1, starting transfers between devices, shards(): other = lax.ppermute(send, 'c', [(0, 1), (1, 0)])  6.49 us
    pallas_call x1, Pallas kernels, shards(): pl.pallas_call(grad_kernel, out_shape=(like(COLS, TOK, DK), like(COLS, TO...  4.78 us
    pallas_call x1, Pallas kernels, shards(): pl.pallas_call(chunk_kernel, out_shape=(like(COLS, DK + 2 * SLICE, DK), l...  4.69 us
    pallas_call x1, Pallas kernels, shards(): pl.pallas_call(row_kernel, out_shape=(like(ROWS * COLS, 3 * SLICE, DK), l...  3.57 us
  transfers between devices with their start and end apart: 2, of which 2 were waited for; matrix products, arithmetic and copies ran while one was open for 1% of the time, Pallas kernels for 0%

profile of v1, /device:TPU:1, one launch (start us, length us, event | category | flops | bytes accessed | tf_op | source)
XLA Modules:
  0.0 104.0 jit_solution(14175096348512721279)
XLA Ops:
  0.0 1.3 %copy.8.head_ref = f32[2,1]{1,0:T(2,128)} copy(f32[2,1]{0,1:T(1,128)} %param.9) | data formatting | bytes 16 | tf_op args[3]
  1.3 4.7 %chunk.1 = (f32[8,160,128]{2,1,0:T(8,128)}, f32[6,128,128]{2,1,0:T(8,128)}) custom-call(bf16[3,128,128]{2,1,0:T(8,128)(2,1)} %proj_ref.3, bf16[128,128]{1,0:T(8,128)(2,1)} %grad_ref.3, f32[2,1,128]{2,1,0:T(1,128)} %logit_ref.3, f32[2,1]{1,0:T(2,128)} %copy.8.head_ref), custom_call_target="tpu_custom_call" | custom-call | tf_op jit(solution)/shard_map/chunk/pallas_call | solution.py:302
  6.0 0.0 copy-start.1
  6.0 24.6 %all_to_all.15.in_ref = f32[8,160,128]{2,1,0:T(8,128)} all-to-all(f32[8,160,128]{2,1,0:T(8,128)} %get-tuple-element.12), channel_id=1, replica_groups=mesh['x'=4,'y'=8,'z'=8,'c'=2] {'y'}, dimensions={0} | all-to-all | bytes 1310720 | tf_op jit(solution)/shard_map/all_to_all | solution.py:309
  30.6 3.6 %row.1 = (f32[32,48,128]{2,1,0:T(8,128)}, f32[2,128,128]{2,1,0:T(8,128)}) custom-call(f32[8,160,128]{2,1,0:T(8,128)} %all_to_all.15.in_ref), custom_call_target="tpu_custom_call" | custom-call | tf_op jit(solution)/shard_map/row/pallas_call | solution.py:310
  34.2 7.9 %all-to-all-start.1 = ((f32[32,48,128]{2,1,0:T(8,128)}), f32[32,48,128]{2,1,0:T(8,128)S(1)}, u32[]{:S(2)}, u32[]{:S(2)}) async-start(f32[32,48,128]{2,1,0:T(8,128)} %get-tuple-element.14), calls=%async_computation.1 | async-start | bytes 1572864 | tf_op jit(solution)/shard_map/all_to_all | solution.py:318
  42.1 0.0 copy-done.1
  42.1 0.6 copy.9.gate_ref
  42.7 19.1 %all-to-all-done.1.in_ref = f32[32,48,128]{2,1,0:T(8,128)S(1)} async-done(((f32[32,48,128]{2,1,0:T(8,128)}), f32[32,48,128]{2,1,0:T(8,128)S(1)}, u32[]{:S(2)}, u32[]{:S(2)}) %all-to-all-start.1) | async-done | bytes 786464 | tf_op jit(solution)/shard_map/all_to_all | solution.py:318
  61.8 0.0 copy-start
  61.8 0.9 copy-done
  62.7 4.8 %grad.1 = (f32[8,128,128]{2,1,0:T(8,128)}, f32[8,128,128]{2,1,0:T(8,128)}) custom-call(bf16[3,128,128]{2,1,0:T(8,128)(2,1)} %proj_ref.3, bf16[128,128]{1,0:T(8,128)(2,1)} %grad_ref.3, f32[2,1,128]{2,1,0:T(1,128)} %logit_ref.3, f32[2,1]{1,0:T(2,128)} %copy.8.head_ref, bf16[3,2048,128]{2,1,0:T(8,128)(2,1)} %weight_hbm.1, bf16[2,1,2048]{2,1,0:T(2,128)(2,1)} %copy.9.gate_ref, ...), custom_call_target="tpu_custom_call" | custom-call | tf_op jit(solution)/shard_map/grad/pallas_call | solution.py:319
  67.5 6.5 %collective-permute-start = (f32[8,128,128]{2,1,0:T(8,128)}, f32[8,128,128]{2,1,0:T(8,128)S(1)}, u32[]{:S(2)}, u32[]{:S(2)}) collective-permute-start(f32[8,128,128]{2,1,0:T(8,128)} %get-tuple-element.16), channel_id=1, source_target_pairs={{0,1},{1,0},{2,3},{3,2},{4,5},{5,4},{6,7},{7,6},{8,9},{9,8},{10,11... | collective-permute-start | bytes 1572872 | tf_op jit(solution)/shard_map/ppermute | solution.py:330
  74.0 1.7 %collective-permute-done = f32[8,128,128]{2,1,0:T(8,128)S(1)} collective-permute-done((f32[8,128,128]{2,1,0:T(8,128)}, f32[8,128,128]{2,1,0:T(8,128)S(1)}, u32[]{:S(2)}, u32[]{:S(2)}) %collective-permute-start) | collective-permute-done | bytes 524320 | tf_op jit(solution)/shard_map/ppermute | solution.py:330
  75.7 1.1 %add.3 = f32[8,128,128]{2,1,0:T(8,128)S(1)} add(f32[8,128,128]{2,1,0:T(8,128)} %get-tuple-element.15, f32[8,128,128]{2,1,0:T(8,128)S(1)} %collective-permute-done) | non-fusion elementwise | flops 131072 | bytes 1572864 | tf_op jit(solution)/shard_map/add | solution.py:331
  76.8 26.6 %all_to_all.16 = f32[8,128,128]{2,1,0:T(8,128)S(1)} all-to-all(f32[8,128,128]{2,1,0:T(8,128)S(1)} %add.3), channel_id=1, replica_groups=mesh['x'=4,'y'=8,'z'=8,'c'=2] {'z'}, dimensions={0} | all-to-all | bytes 1048576 | tf_op jit(solution)/shard_map/all_to_all | solution.py:331
  103.4 0.6 reduce_sum.9
Async XLA Ops:
  6.0 36.1 %copy-start.1 = (bf16[2,1,2048]{2,0,1:T(2,128)(2,1)S(1)}, bf16[2,1,2048]{2,0,1:T(2,128)(2,1)}, u32[]{:S(2)}) copy-start(bf16[2,1,2048]{2,0,1:T(2,128)(2,1)} %param.11) | copy-start | bytes 24580
  34.2 27.6 %all-to-all-start.1 = ((f32[32,48,128]{2,1,0:T(8,128)}), f32[32,48,128]{2,1,0:T(8,128)S(1)}, u32[]{:S(2)}, u32[]{:S(2)}) async-start(f32[32,48,128]{2,1,0:T(8,128)} %get-tuple-element.14), calls=%async_computation.1 | async-start | bytes 1572864 | tf_op jit(solution)/shard_map/all_to_all | solution.py:318
  61.8 0.9 copy-start
  67.5 8.2 %collective-permute-start = (f32[8,128,128]{2,1,0:T(8,128)}, f32[8,128,128]{2,1,0:T(8,128)S(1)}, u32[]{:S(2)}, u32[]{:S(2)}) collective-permute-start(f32[8,128,128]{2,1,0:T(8,128)} %get-tuple-element.16), channel_id=1, source_target_pairs={{0,1},{1,0},{2,3},{3,2},{4,5},{5,4},{6,7},{7,6},{8,9},{9,8},{10,11... | collective-permute-start | bytes 1572872 | tf_op jit(solution)/shard_map/ppermute | solution.py:330

commit v2 on v1

--- a/solution.py
+++ b/solution.py
@@ -11,8 +11,10 @@
 ROWS = 4
 COLS = 8
 SLICE = DK // COLS
+ORDER = (7, 5, 3, 6, 4, 2, 1, 0)
 SCALE = DK ** (-0.5)
 F32 = jnp.float32
+CHUNK_LIMIT = 60 << 20
 
 NN = (((1,), (0,)), ((), ()))
 NT = (((1,), (1,)), ((), ()))
@@ -54,8 +56,9 @@
 
 
 def gates(logit_ref, head_ref, row, col):
-    rate = jnp.exp(jnp.full((1, TOK), head_ref[0, 0], F32))
-    shifted = logit_ref[0] + head_ref[1, 0]
+    heads = head_ref[...]
+    rate = jnp.exp(heads[:, 0:1])
+    shifted = logit_ref[0] + heads[:, 1:2]
     soft = jnp.maximum(shifted, 0.0) + jnp.log1p(jnp.exp(-jnp.abs(shifted)))
     decay_row = -rate * soft
     cumul = lane_sum(jnp.where(col <= row, decay_row, 0.0))
@@ -84,7 +87,30 @@
     return out
 
 
-def chunk_kernel(proj_ref, grad_ref, logit_ref, head_ref, out_ref, saved_ref):
+def chunk_kernel(
+    proj_hbm,
+    grad_hbm,
+    logit_hbm,
+    head_hbm,
+    out_ref,
+    saved_ref,
+    proj_ref,
+    grad_ref,
+    logit_ref,
+    head_ref,
+    sems,
+):
+    pairs = (
+        (logit_hbm, logit_ref),
+        (head_hbm, head_ref),
+        (proj_hbm, proj_ref),
+        (grad_hbm, grad_ref),
+    )
+    copies = [pltpu.make_async_copy(*pair, sems.at[i]) for i, pair in enumerate(pairs)]
+    for copy in copies:
+        copy.start()
+    for copy in copies:
+        copy.wait()
     row, col = iotas()
     grown, rest, total, write, ratio, _ = gates(logit_ref, head_ref, row, col)
     queries = unit(proj_ref[0].astype(F32))[0] * SCALE
@@ -176,13 +202,14 @@
 
     scratch_ref[...] = whole[0]
     piece = scratch_ref[pl.ds(pl.multiple_of(here_y * SLICE, SLICE), SLICE)]
+    at_x = jnp.full((SLICE, DK), here_x, jnp.int32)
     for peer_x in range(ROWS):
-        own = jnp.full((SLICE, DK), here_x, jnp.int32) == peer_x
+        own = at_x == peer_x
+        sent = jnp.where(at_x < peer_x, whole[1], whole[2])
         for peer_y in range(COLS):
             slot = peer_x * COLS + peer_y
-            out_ref[slot, :SLICE] = piece
-            out_ref[slot, SLICE : 2 * SLICE] = jnp.where(own, prefix[peer_y], whole[1])
-            out_ref[slot, 2 * SLICE :] = jnp.where(own, suffix[peer_y], whole[2])
+            out_ref[slot, :SLICE] = jnp.where(own, prefix[peer_y], piece)
+            out_ref[slot, SLICE:] = jnp.where(own, suffix[peer_y], sent)
 
 
 def grad_kernel(
@@ -190,18 +217,15 @@
     grad_ref,
     logit_ref,
     head_ref,
-    weight_hbm,
+    weight_ref,
     gate_ref,
     saved_ref,
     own_ref,
     in_ref,
-    keep_ref,
     send_ref,
-    weight_ref,
-    sem,
+    low_ref,
+    slope_ref,
 ):
-    fetch = pltpu.make_async_copy(weight_hbm, weight_ref, sem)
-    fetch.start()
     here_x = lax.axis_index("x")
     here_c = lax.axis_index("c")
 
@@ -209,18 +233,18 @@
         rows = pl.ds(row_at * COLS, COLS)
         return in_ref[rows, kind * SLICE : (kind + 1) * SLICE].reshape(DK, DK)
 
-    step1, step2 = part(1, 0), part(2, 0)
+    step1, step2 = halves(part(1, 0)), halves(part(2, 0))
     s1 = part(0, 1)
     s2 = dot(s1, step1) + part(1, 1)
     s3 = dot(s2, step2) + part(2, 1)
-    g2 = part(3, 2)
-    g1 = dot(g2, step2, NT) + part(2, 2)
-    g0 = dot(g1, step1, NT) + part(1, 2)
+    g2 = part(3, 1)
+    g1 = dot(g2, step2, NT) + part(2, 1)
+    g0 = dot(g1, step1, NT) + part(1, 1)
     zero = jnp.zeros((DK, DK), F32)
     s_row = jnp.where(here_x == 0, zero, jnp.where(here_x == 1, s1, jnp.where(here_x == 2, s2, s3)))
     g_row = jnp.where(here_x == 3, zero, jnp.where(here_x == 2, g2, jnp.where(here_x == 1, g1, g0)))
-    state = dot(s_row, own_ref[0]) + part(here_x, 1)
-    later = dot(g_row, own_ref[1], NT) + part(here_x, 2)
+    state = dot(s_row, own_ref[0]) + part(here_x, 0)
+    later = dot(g_row, own_ref[1], NT) + part(here_x, 1)
 
     row, col = iotas()
     grown, rest, total, write, ratio, slope = gates(logit_ref, head_ref, row, col)
@@ -274,62 +298,122 @@
     grad_q = q_scale * (d_queries - q_unit * lane_sum(q_unit * d_queries))
     grad_k = k_scale * (d_keys - keys * lane_sum(keys * d_keys))
     grad_v = write * pulled
-    low_qk = jnp.concatenate([grad_q, grad_k], 1).astype(jnp.bfloat16)
-    low_v = grad_v.astype(jnp.bfloat16)
-
-    fetch.wait()
-    for peer in range(COLS):
-        rows = pl.ds(peer * 2 * DK, 2 * DK)
-        weights = jnp.concatenate([weight_ref[0, rows], weight_ref[1, rows]], 1)
-        acc = lax.dot_general(low_qk, weights, NT, preferred_element_type=F32)
-        acc = acc + lax.dot_general(low_v, weight_ref[2, rows], NT, preferred_element_type=F32)
-        acc = acc + d_logit0 * gate_ref[0, :, rows].astype(F32)
-        acc = acc + d_logit1 * gate_ref[1, :, rows].astype(F32)
-        keep_ref[peer] = jnp.where(here_c == 0, acc[:, :DK], acc[:, DK:])
-        send_ref[peer] = jnp.where(here_c == 0, acc[:, DK:], acc[:, :DK])
+    low = [grad.astype(BF16) for grad in (grad_q, grad_k, grad_v)]
+    for source in range(3):
+        low_ref[source] = low[source]
+    slopes = (d_logit0, d_logit1)
+    slope_ref[...] = jnp.where(col == 0, d_logit0, d_logit1)
+    for slot, peer in enumerate(ORDER):
+        send_ref[slot] = projected_to(2 * peer + 1 - here_c, low, slopes, weight_ref, gate_ref)
+
+
+def projected_to(head, low, slopes, weight_ref, gate_ref):
+    at = pl.multiple_of(head * DK, DK)
+    rows = pl.ds(at, DK)
+    weights = jnp.concatenate([weight_ref[0, rows], weight_ref[1, rows]], 1)
+    acc = lax.dot_general(
+        jnp.concatenate(low[:2], 1), weights, NT, preferred_element_type=F32
+    ) + lax.dot_general(low[2], weight_ref[2, rows], NT, preferred_element_type=F32)
+    for kind in range(2):
+        acc = acc + slopes[kind] * gate_ref[kind : kind + 1, rows].astype(F32)
+    return acc
+
+
+def keep_kernel(low_ref, slope_ref, weight_ref, gate_ref, other_ref, out_ref):
+    here_c = lax.axis_index("c")
+    low = [low_ref[source] for source in range(3)]
+    slopes = (slope_ref[:, 0:1], slope_ref[:, 1:2])
+    for slot, peer in enumerate(ORDER):
+        own = projected_to(2 * peer + here_c, low, slopes, weight_ref, gate_ref)
+        out_ref[slot] = other_ref[slot] + own
 
 
 VMEM = pl.BlockSpec(memory_space=pltpu.VMEM)
-SMEM = pl.BlockSpec(memory_space=pltpu.SMEM)
-ANY = pl.BlockSpec(memory_space=pl.ANY)
+HBM = pl.BlockSpec(memory_space=pltpu.HBM)
 
 
 def like(*shape):
     return jax.ShapeDtypeStruct(shape, F32)
 
 
+def call(kernel, name, out_shape, in_specs, *args, scratch=(), limit=16 << 20):
+    return pl.pallas_call(
+        kernel,
+        out_shape=out_shape,
+        in_specs=in_specs,
+        out_specs=jax.tree.map(lambda _: VMEM, out_shape),
+        scratch_shapes=scratch,
+        compiler_params=pltpu.CompilerParams(vmem_limit_bytes=limit),
+        name=name,
+    )(*args)
+
+
 def shards(projected, out_grad, logits, head_params, qkv_weight, gate_weight):
-    chunks, saved = pl.pallas_call(
+    heads = head_params.T
+    gate = jnp.transpose(gate_weight, (1, 0, 2))[0]
+    chunks, saved = call(
         chunk_kernel,
-        out_shape=(like(COLS, DK + 2 * SLICE, DK), like(6, DK, DK)),
-        in_specs=[VMEM, VMEM, VMEM, SMEM],
-        out_specs=(VMEM, VMEM),
-        name="chunk",
-    )(projected, out_grad, logits, head_params)
+        "chunk",
+        (like(COLS, DK + 2 * SLICE, DK), like(6, DK, DK)),
+        [HBM] * 4,
+        projected,
+        out_grad,
+        logits,
+        heads,
+        scratch=[
+            pltpu.VMEM((3, TOK, DK), BF16),
+            pltpu.VMEM((TOK, DK), BF16),
+            pltpu.VMEM((2, 1, TOK), F32),
+            pltpu.VMEM((1, 2), F32),
+            pltpu.SemaphoreType.DMA((4,)),
+        ],
+        limit=CHUNK_LIMIT,
+    )
     chunks = lax.all_to_all(chunks, "y", 0, 0, tiled=True)
-    rows, own = pl.pallas_call(
+    rows, own = call(
         row_kernel,
-        out_shape=(like(ROWS * COLS, 3 * SLICE, DK), like(2, DK, DK)),
-        in_specs=[VMEM],
-        out_specs=(VMEM, VMEM),
-        scratch_shapes=[pltpu.VMEM((DK, DK), F32)],
-        name="row",
-    )(chunks)
+        "row",
+        (like(ROWS * COLS, 2 * SLICE, DK), like(2, DK, DK)),
+        [VMEM],
+        chunks,
+        scratch=[pltpu.VMEM((DK, DK), F32)],
+    )
     rows = lax.all_to_all(rows, ("x", "y"), 0, 0, tiled=True)
-    keep, send = pl.pallas_call(
+    send, low, slopes = call(
         grad_kernel,
-        out_shape=(like(COLS, TOK, DK), like(COLS, TOK, DK)),
-        in_specs=[VMEM, VMEM, VMEM, SMEM, ANY, VMEM, VMEM, VMEM, VMEM],
-        out_specs=(VMEM, VMEM),
-        scratch_shapes=[
-            pltpu.VMEM((3, 2048, DK), jnp.bfloat16),
-            pltpu.SemaphoreType.DMA(()),
-        ],
-        name="grad",
-    )(projected, out_grad, logits, head_params, qkv_weight, gate_weight, saved, own, rows)
+        "grad",
+        (
+            like(COLS, TOK, DK),
+            jax.ShapeDtypeStruct((3, TOK, DK), BF16),
+            like(TOK, DK),
+        ),
+        [VMEM] * 9,
+        projected,
+        out_grad,
+        logits,
+        heads,
+        qkv_weight,
+        gate,
+        saved,
+        own,
+        rows,
+    )
     other = lax.ppermute(send, "c", [(0, 1), (1, 0)])
-    summed = lax.all_to_all(keep + other, "z", 0, 0, tiled=True)
-    return summed.sum(axis=0).astype(jnp.bfloat16)
+    part = call(
+        keep_kernel,
+        "keep",
+        like(COLS, TOK, DK),
+        [VMEM] * 5,
+        low,
+        slopes,
+        qkv_weight,
+        gate,
+        other,
+    )
+    summed = lax.all_to_all(
+        part, "z", 0, 0, tiled=True, axis_index_groups=[list(ORDER)]
+    )
+    return summed.sum(axis=0).astype(BF16)
 
 
 def solution(mesh):

time: 105 us -> 88.9 us (0.85)
  waiting for transfers between devices: 20.8 us -> 1.51 us
  blocking collectives: 51.2 us -> 70.2 us
  starting transfers between devices: 14.4 us -> 5.62 us
  Pallas kernels: 13 us -> 9.19 us
  local copies, waits for them, and re-layouts: 2.83 us -> 0.03 us
  other arithmetic: 1.77 us -> 0.64 us
    all_to_all x1 -> x0, waiting for transfers between devices: 19.1 us -> none  [shards(): rows = lax.all_to_all(rows, ('x', 'y'), 0, 0, tiled=True)]
    all_to_all x1 -> x2, blocking collectives: 26.6 us -> 44.9 us  [the longest x1 23.8 us: shards(): lax.all_to_all(part, 'z', 0, 0, tiled=True, axis_index_groups=[list(ORDER)])]
    all_to_all x1 -> x0, starting transfers between devices: 7.89 us -> none  [shards(): rows = lax.all_to_all(rows, ('x', 'y'), 0, 0, tiled=True)]
    pallas_call x3 -> x4, Pallas kernels: 13 us -> 9.19 us  [call(): pl.pallas_call(kernel, out_shape=out_shape, in_specs=in_specs, out_specs=...]
    unnamed x6 -> x14, local copies, waits for them, and re-layouts: 2.83 us -> 0.03 us
    add x1 -> x0, other arithmetic: 1.12 us -> none  [shards(): summed = lax.all_to_all(keep + other, 'z', 0, 0, tiled=True)]
  transfers between devices with their start and end apart: 2 -> 1, of which waited for: 2 -> 1; matrix products, arithmetic and copies ran while one was open for 1% -> 0% of each run, Pallas kernels for 0% -> 0%
where the time goes in v2:
time: 88.9 us; the launch traced here: 87.3 us
  blocking collectives  70.2 us (79%)
  Pallas kernels  9.19 us (10%)
  starting transfers between devices  5.62 us (6%)
  waiting for transfers between devices  1.51 us (2%)
    all_to_all x1, blocking collectives, shards(): chunks = lax.all_to_all(chunks, 'y', 0, 0, tiled=True)  25.2 us
    all_to_all x1, blocking collectives, shards(): lax.all_to_all(part, 'z', 0, 0, tiled=True, axis_index_groups=[list(ORDER)])  23.8 us
    all_to_all x1, blocking collectives, shards(): rows = lax.all_to_all(rows, ('x', 'y'), 0, 0, tiled=True)  21.1 us
    pallas_call x4, Pallas kernels, call(): pl.pallas_call(kernel, out_shape=out_shape, in_specs=in_specs, out_specs=...  9.19 us
    ppermute x1, starting transfers between devices, shards(): other = lax.ppermute(send, 'c', [(0, 1), (1, 0)])  5.62 us
  transfers between devices with their start and end apart: 1, of which 1 were waited for; matrix products, arithmetic and copies ran while one was open for 0% of the time, Pallas kernels for 0%

profile of v2, /device:TPU:1, one launch (start us, length us, event | category | flops | bytes accessed | tf_op | source)
XLA Modules:
  0.0 87.3 jit_solution(16551785990076232651)
XLA Ops:
  0.0 0.0 copy-start
  0.0 0.0 copy-start.1
  0.0 0.0 copy-start.3
  0.0 0.0 copy-start.4
  0.0 0.0 copy-start.5
  0.0 0.0 copy-start.6
  0.0 4.8 %chunk.1 = (f32[8,160,128]{2,1,0:T(8,128)}, f32[6,128,128]{2,1,0:T(8,128)}) custom-call(bf16[3,128,128]{2,1,0:T(8,128)(2,1)} %proj_ref.1, bf16[128,128]{1,0:T(8,128)(2,1)} %grad_ref.1, f32[2,1,128]{2,1,0:T(1,128)} %logit_ref.1, f32[1,2]{1,0:T(1,128)} %bitcast.4), custom_call_target="tpu_custom_call" | custom-call | tf_op jit(solution)/shard_map/chunk/pallas_call | solution.py:340
  4.9 0.0 copy-start.2
  4.9 25.2 %all_to_all.15.in_ref = f32[8,160,128]{2,1,0:T(8,128)S(1)} all-to-all(f32[8,160,128]{2,1,0:T(8,128)} %get-tuple-element.13), channel_id=1, replica_groups=mesh['x'=4,'y'=8,'z'=8,'c'=2] {'y'}, dimensions={0} | all-to-all | bytes 1310720 | tf_op jit(solution)/shard_map/all_to_all | solution.py:372
  30.1 1.8 %row.1 = (f32[32,32,128]{2,1,0:T(8,128)S(1)}, f32[2,128,128]{2,1,0:T(8,128)S(1)}) custom-call(f32[8,160,128]{2,1,0:T(8,128)S(1)} %all_to_all.15.in_ref), custom_call_target="tpu_custom_call" | custom-call | tf_op jit(solution)/shard_map/row/pallas_call | solution.py:340
  32.0 21.1 %all_to_all.16.in_ref = f32[32,32,128]{2,1,0:T(8,128)S(1)} all-to-all(f32[32,32,128]{2,1,0:T(8,128)S(1)} %get-tuple-element.15), channel_id=1, replica_groups=mesh['x'=4,'y'=8,'z'=8,'c'=2] {'x','y'}, dimensions={0} | all-to-all | bytes 1048576 | tf_op jit(solution)/shard_map/all_to_all | solution.py:381
  53.1 0.0 copy-done
  53.1 0.0 copy-done.1
  53.1 0.0 copy-done.3
  53.1 0.0 copy-done.4
  53.1 0.0 copy-done.5
  53.1 0.0 copy-done.6
  53.1 0.0 copy-done.2
  53.1 2.1 %grad.1 = (f32[8,128,128]{2,1,0:T(8,128)S(1)}, bf16[3,128,128]{2,1,0:T(8,128)(2,1)S(1)}, f32[128,128]{1,0:T(8,128)S(1)}) custom-call(bf16[3,128,128]{2,1,0:T(8,128)(2,1)S(1)} %copy-done.1, bf16[128,128]{1,0:T(8,128)(2,1)S(1)} %copy-done.3, f32[2,1,128]{2,1,0:T(1,128)S(1)} %copy-done.5, f32[1,2]{1,0:T(1,128)S(1)} %bitcast.5, ...), custom_call_target="tpu_custom_call" | custom-call | tf_op jit(solution)/shard_map/grad/pallas_call | solution.py:340
  55.2 5.6 %collective-permute-start = (f32[8,128,128]{2,1,0:T(8,128)S(1)}, f32[8,128,128]{2,1,0:T(8,128)S(1)}, u32[]{:S(2)}, u32[]{:S(2)}) collective-permute-start(f32[8,128,128]{2,1,0:T(8,128)S(1)} %get-tuple-element.18), channel_id=1, source_target_pairs={{0,1},{1,0},{2,3},{3,2},{4,5},{5,4},{6,7},{7,6},{8,9},{9,8},{10,11... | collective-permute-start | bytes 1572872 | tf_op jit(solution)/shard_map/ppermute | solution.py:401
  60.8 1.5 %collective-permute-done.other_ref = f32[8,128,128]{2,1,0:T(8,128)S(1)} collective-permute-done((f32[8,128,128]{2,1,0:T(8,128)S(1)}, f32[8,128,128]{2,1,0:T(8,128)S(1)}, u32[]{:S(2)}, u32[]{:S(2)}) %collective-permute-start) | collective-permute-done | bytes 524320 | tf_op jit(solution)/shard_map/ppermute | solution.py:401
  62.3 0.5 keep.1
  62.8 23.8 %all_to_all.17 = f32[8,128,128]{2,1,0:T(8,128)S(1)} all-to-all(f32[8,128,128]{2,1,0:T(8,128)S(1)} %keep.1), channel_id=1, replica_groups={{14,10,6,12,8,4,2,0},{15,11,7,13,9,5,3,1},{30,26,22,28,24,20,18,16},{31..., dimensions={0} | all-to-all | bytes 1048576 | tf_op jit(solution)/shard_map/all_to_all | solution.py:413
  86.6 0.6 reduce_sum.9
Async XLA Ops:
  0.0 53.1 %copy-start = (bf16[3,2048,128]{2,1,0:T(8,128)(2,1)S(1)}, bf16[3,2048,128]{2,1,0:T(8,128)(2,1)}, u32[]{:S(2)}) copy-start(bf16[3,2048,128]{2,1,0:T(8,128)(2,1)} %weight_ref.3) | copy-start | bytes 4718596
  0.0 53.1 %copy-start.1 = (bf16[3,128,128]{2,1,0:T(8,128)(2,1)S(1)}, bf16[3,128,128]{2,1,0:T(8,128)(2,1)}, u32[]{:S(2)}) copy-start(bf16[3,128,128]{2,1,0:T(8,128)(2,1)} %proj_ref.1) | copy-start | bytes 294916
  0.0 53.1 %copy-start.3 = (bf16[128,128]{1,0:T(8,128)(2,1)S(1)}, bf16[128,128]{1,0:T(8,128)(2,1)}, u32[]{:S(2)}) copy-start(bf16[128,128]{1,0:T(8,128)(2,1)} %grad_ref.1) | copy-start | bytes 98308
  0.0 53.1 %copy-start.4 = (bf16[2,1,2048]{2,0,1:T(2,128)(2,1)S(1)}, bf16[2,1,2048]{2,0,1:T(2,128)(2,1)}, u32[]{:S(2)}) copy-start(bf16[2,1,2048]{2,0,1:T(2,128)(2,1)} %param.11) | copy-start | bytes 24580
  0.0 53.1 %copy-start.5 = (f32[2,1,128]{2,1,0:T(1,128)S(1)}, f32[2,1,128]{2,1,0:T(1,128)}, u32[]{:S(2)}) copy-start(f32[2,1,128]{2,1,0:T(1,128)} %logit_ref.1) | copy-start | bytes 3076
  0.0 53.1 %copy-start.6 = (f32[2,1]{0,1:T(1,128)S(1)}, f32[2,1]{0,1:T(1,128)}, u32[]{:S(2)}) copy-start(f32[2,1]{0,1:T(1,128)} %param.9) | copy-start | bytes 28
  4.9 48.2 %copy-start.2 = (f32[6,128,128]{2,1,0:T(8,128)S(1)}, f32[6,128,128]{2,1,0:T(8,128)}, u32[]{:S(2)}) copy-start(f32[6,128,128]{2,1,0:T(8,128)} %get-tuple-element.12.saved_ref) | copy-start | bytes 1179652
  55.2 7.1 %collective-permute-start = (f32[8,128,128]{2,1,0:T(8,128)S(1)}, f32[8,128,128]{2,1,0:T(8,128)S(1)}, u32[]{:S(2)}, u32[]{:S(2)}) collective-permute-start(f32[8,128,128]{2,1,0:T(8,128)S(1)} %get-tuple-element.18), channel_id=1, source_target_pairs={{0,1},{1,0},{2,3},{3,2},{4,5},{5,4},{6,7},{7,6},{8,9},{9,8},{10,11... | collective-permute-start | bytes 1572872 | tf_op jit(solution)/shard_map/ppermute | solution.py:401

commit v3 on v2

--- a/solution.py
+++ b/solution.py
@@ -12,6 +12,7 @@
 COLS = 8
 SLICE = DK // COLS
 ORDER = (7, 5, 3, 6, 4, 2, 1, 0)
+GRID_ORDER = tuple(x * COLS + y for y in reversed(range(COLS)) for x in range(ROWS))
 SCALE = DK ** (-0.5)
 F32 = jnp.float32
 CHUNK_LIMIT = 60 << 20
@@ -31,13 +32,23 @@
     return high, (x - high.astype(F32)).astype(BF16)
 
 
+def whole(pair):
+    return pair[0].astype(F32) + pair[1].astype(F32)
+
+
 def dot(left, right, dims=NN):
     (lh, ll), (rh, rl) = halves(left), halves(right)
-
-    def one(a, b):
-        return lax.dot_general(a, b, dims, preferred_element_type=F32)
-
-    return one(lh, rh) + (one(lh, rl) + one(ll, rh))
+    (lk,), (rk,) = dims[0]
+    both = jnp.concatenate([lh, ll], lk)
+    if rh.shape[1 - rk] == DK:
+        first = jnp.concatenate([rh, rh], rk)
+        second = jnp.concatenate([rl, jnp.zeros_like(rl)], rk)
+        out = lax.dot_general(
+            both, jnp.concatenate([first, second], 1 - rk), dims, preferred_element_type=F32
+        )
+        return out[:, :DK] + out[:, DK:]
+    out = lax.dot_general(both, jnp.concatenate([rh, rh], rk), dims, preferred_element_type=F32)
+    return out + lax.dot_general(lh, rl, dims, preferred_element_type=F32)
 
 
 def iotas():
@@ -73,17 +84,20 @@
 
 def inverse_of(strict, row, col):
     eye = jnp.where(row == col, 1.0, 0.0).astype(F32)
-    near = jnp.where((row >> 3) == (col >> 3), strict, 0.0)
-    power2 = dot(near, near)
-    out = eye - near
-    both = dot(jnp.concatenate([out, power2], 0), power2)
-    out, power4 = out + both[:TOK], both[TOK:]
-    out = out + dot(out, power4)
-    for level in (3, 4, 5, 6):
-        joined = ((row >> (level + 1)) == (col >> (level + 1))) & ((row >> level) != (col >> level))
-        off = jnp.where(joined, strict, 0.0)
-        pair = halves(out)
-        out = out - dot(pair, dot(off, pair))
+
+    def same(level):
+        return (row >> level) == (col >> level)
+
+    out = eye - jnp.where(same(1), strict, 0.0)
+    for low, high in ((1, 4), (4, 7)):
+        near = halves(out)
+        off = jnp.where(same(high) & ~same(low), strict, 0.0)
+        power = dot(near, off)
+        both = dot(power, jnp.concatenate([power, out], 1))
+        power, out = both[:, :TOK], out - both[:, TOK:]
+        both = dot(power, jnp.concatenate([power, out], 1))
+        power, out = both[:, :TOK], out + both[:, TOK:]
+        out = out + dot(power, out)
     return out
 
 
@@ -92,13 +106,17 @@
     grad_hbm,
     logit_hbm,
     head_hbm,
-    out_ref,
-    saved_ref,
+    out_hbm,
+    saved_hbm,
     proj_ref,
     grad_ref,
     logit_ref,
     head_ref,
-    sems,
+    step_ref,
+    edge_ref,
+    saved_ref,
+    in_sems,
+    out_sems,
 ):
     pairs = (
         (logit_hbm, logit_ref),
@@ -106,11 +124,22 @@
         (proj_hbm, proj_ref),
         (grad_hbm, grad_ref),
     )
-    copies = [pltpu.make_async_copy(*pair, sems.at[i]) for i, pair in enumerate(pairs)]
+    copies = [pltpu.make_async_copy(*pair, in_sems.at[i]) for i, pair in enumerate(pairs)]
     for copy in copies:
         copy.start()
     for copy in copies:
         copy.wait()
+    leaving = []
+
+    def leave(source, target):
+        copy = pltpu.make_async_copy(source, target, out_sems.at[len(leaving)])
+        copy.start()
+        leaving.append(copy)
+
+    def save(at, value):
+        saved_ref[at] = value
+        leave(saved_ref.at[at], saved_hbm.at[at])
+
     row, col = iotas()
     grown, rest, total, write, ratio, _ = gates(logit_ref, head_ref, row, col)
     queries = unit(proj_ref[0].astype(F32))[0] * SCALE
@@ -121,24 +150,29 @@
     bare = jnp.where(row > col, ratio * inner[:TOK], 0.0)
     attend = ratio * inner[TOK:]
     inverse = inverse_of(bare * write, row, col)
+    attended = dot(attend, out_grad, TN)
+    direct = dot(out_grad, grown * queries, TN)
     solved = dot(inverse, jnp.concatenate([(write * grown) * keys, write * values], 1))
     key_weights, base = solved[:, :DK], solved[:, DK:]
     rest_keys = rest * keys
     moved = dot(solved, rest_keys, TN)
     eye = jnp.where(row == col, 1.0, 0.0).astype(F32)
-    step = total * eye - moved[:DK]
-    offset = moved[DK:]
-    back = dot(out_grad, grown * queries - dot(attend, key_weights), TN)
+    step_ref[...] = total * eye - moved[:DK]
     for peer in range(COLS):
-        out_ref[peer, :DK] = step
-        out_ref[peer, DK : DK + SLICE] = offset[peer * SLICE : (peer + 1) * SLICE]
-        out_ref[peer, DK + SLICE :] = back[peer * SLICE : (peer + 1) * SLICE]
-    saved_ref[0] = inverse.T
-    saved_ref[1] = key_weights
-    saved_ref[2] = base
-    saved_ref[3] = attend
-    saved_ref[4] = bare
-    saved_ref[5] = dot(attend, out_grad, TN)
+        leave(step_ref, out_hbm.at[peer, pl.ds(0, DK)])
+    back = direct - dot(attended, key_weights, TN)
+    for peer in range(COLS):
+        edge_ref[peer, :SLICE] = moved[DK + peer * SLICE : DK + (peer + 1) * SLICE]
+        edge_ref[peer, SLICE:] = back[peer * SLICE : (peer + 1) * SLICE]
+    leave(edge_ref, out_hbm.at[:, pl.ds(DK, 2 * SLICE)])
+    save(0, inverse.T)
+    save(1, key_weights)
+    save(2, base)
+    save(3, attend)
+    save(4, bare)
+    save(5, attended)
+    for copy in leaving:
+        copy.wait()
 
 
 def row_kernel(in_ref, out_ref, own_ref, scratch_ref):
@@ -207,7 +241,7 @@
         own = at_x == peer_x
         sent = jnp.where(at_x < peer_x, whole[1], whole[2])
         for peer_y in range(COLS):
-            slot = peer_x * COLS + peer_y
+            slot = (COLS - 1 - peer_y) * ROWS + peer_x
             out_ref[slot, :SLICE] = jnp.where(own, prefix[peer_y], piece)
             out_ref[slot, SLICE:] = jnp.where(own, suffix[peer_y], sent)
 
@@ -230,8 +264,9 @@
     here_c = lax.axis_index("c")
 
     def part(row_at, kind):
-        rows = pl.ds(row_at * COLS, COLS)
-        return in_ref[rows, kind * SLICE : (kind + 1) * SLICE].reshape(DK, DK)
+        span = slice(kind * SLICE, (kind + 1) * SLICE)
+        slots = [(COLS - 1 - y) * ROWS + row_at for y in range(COLS)]
+        return jnp.concatenate([in_ref[slot, span] for slot in slots], 0)
 
     step1, step2 = halves(part(1, 0)), halves(part(2, 0))
     s1 = part(0, 1)
@@ -243,8 +278,8 @@
     zero = jnp.zeros((DK, DK), F32)
     s_row = jnp.where(here_x == 0, zero, jnp.where(here_x == 1, s1, jnp.where(here_x == 2, s2, s3)))
     g_row = jnp.where(here_x == 3, zero, jnp.where(here_x == 2, g2, jnp.where(here_x == 1, g1, g0)))
-    state = dot(s_row, own_ref[0]) + part(here_x, 0)
-    later = dot(g_row, own_ref[1], NT) + part(here_x, 1)
+    state = halves(dot(s_row, own_ref[0]) + part(here_x, 0))
+    later = halves(dot(g_row, own_ref[1], NT) + part(here_x, 1))
 
     row, col = iotas()
     grown, rest, total, write, ratio, slope = gates(logit_ref, head_ref, row, col)
@@ -257,7 +292,7 @@
     attend = saved_ref[3]
     bare = saved_ref[4]
 
-    fresh = saved_ref[2] - dot(saved_ref[1], state, NT)
+    fresh = halves(saved_ref[2] - dot(saved_ref[1], state, NT))
     d_fresh = saved_ref[5] + dot(rest_keys, later, NT)
     pulled = dot(saved_ref[0], d_fresh)
     both = dot(jnp.concatenate([out_grad, pulled], 0), state)
@@ -288,7 +323,7 @@
     )
     d_cumul_row = jnp.sum(jnp.where(row == col, d_cumul, 0.0) - ratio_hit, axis=0, keepdims=True)
     at_end = jnp.sum(rest_hit, axis=0, keepdims=True) + total * jnp.sum(
-        lane_sum(later * state), axis=0, keepdims=True
+        lane_sum(whole(later) * whole(state)), axis=0, keepdims=True
     )
     d_decay = lane_sum(jnp.where(col >= row, d_cumul_row, 0.0)) + at_end
     d_logit0 = d_decay * slope
@@ -336,12 +371,12 @@
     return jax.ShapeDtypeStruct(shape, F32)
 
 
-def call(kernel, name, out_shape, in_specs, *args, scratch=(), limit=16 << 20):
+def call(kernel, name, out_shape, in_specs, *args, scratch=(), limit=16 << 20, space=VMEM):
     return pl.pallas_call(
         kernel,
         out_shape=out_shape,
         in_specs=in_specs,
-        out_specs=jax.tree.map(lambda _: VMEM, out_shape),
+        out_specs=jax.tree.map(lambda _: space, out_shape),
         scratch_shapes=scratch,
         compiler_params=pltpu.CompilerParams(vmem_limit_bytes=limit),
         name=name,
@@ -365,8 +400,13 @@
             pltpu.VMEM((TOK, DK), BF16),
             pltpu.VMEM((2, 1, TOK), F32),
             pltpu.VMEM((1, 2), F32),
+            pltpu.VMEM((DK, DK), F32),
+            pltpu.VMEM((COLS, 2 * SLICE, DK), F32),
+            pltpu.VMEM((6, DK, DK), F32),
             pltpu.SemaphoreType.DMA((4,)),
+            pltpu.SemaphoreType.DMA((COLS + 7,)),
         ],
+        space=HBM,
         limit=CHUNK_LIMIT,
     )
     chunks = lax.all_to_all(chunks, "y", 0, 0, tiled=True)
@@ -378,7 +418,9 @@
         chunks,
         scratch=[pltpu.VMEM((DK, DK), F32)],
     )
-    rows = lax.all_to_all(rows, ("x", "y"), 0, 0, tiled=True)
+    rows = lax.all_to_all(
+        rows, ("x", "y"), 0, 0, tiled=True, axis_index_groups=[list(GRID_ORDER)]
+    )
     send, low, slopes = call(
         grad_kernel,
         "grad",

time: 88.9 us -> 86.3 us (0.971)
  Pallas kernels: 9.19 us -> 7.68 us
  blocking collectives: 70.2 us -> 69.1 us
    pallas_call x4, Pallas kernels: 9.19 us -> 7.68 us  [call(): pl.pallas_call(kernel, out_shape=out_shape, in_specs=in_specs, out_specs=...]
    all_to_all x1, blocking collectives: 21.1 us -> 20.1 us  [shards(): lax.all_to_all(rows, ('x', 'y'), 0, 0, tiled=True, axis_index_groups=[lis...]
where the time goes in v3:
time: 86.3 us; the launch traced here: 85.4 us
  blocking collectives  69.1 us (80%)
  Pallas kernels  7.68 us (9%)
  starting transfers between devices  6.35 us (7%)
  waiting for transfers between devices  1.51 us (2%)
    all_to_all x1, blocking collectives, shards(): chunks = lax.all_to_all(chunks, 'y', 0, 0, tiled=True)  25.2 us
    all_to_all x1, blocking collectives, shards(): lax.all_to_all(part, 'z', 0, 0, tiled=True, axis_index_groups=[list(ORDER)])  23.8 us
    all_to_all x1, blocking collectives, shards(): lax.all_to_all(rows, ('x', 'y'), 0, 0, tiled=True, axis_index_groups=[lis...  20.1 us
    pallas_call x4, Pallas kernels, call(): pl.pallas_call(kernel, out_shape=out_shape, in_specs=in_specs, out_specs=...  7.68 us
    ppermute x1, starting transfers between devices, shards(): other = lax.ppermute(send, 'c', [(0, 1), (1, 0)])  6.35 us
  transfers between devices with their start and end apart: 1, of which 1 were waited for; matrix products, arithmetic and copies ran while one was open for 0% of the time, Pallas kernels for 0%

profile of v3, /device:TPU:1, one launch (start us, length us, event | category | flops | bytes accessed | tf_op | source)
XLA Modules:
  0.0 85.4 jit_solution(9527695664161479647)
XLA Ops:
  0.0 0.0 copy-start
  0.0 0.0 copy-start.1
  0.0 0.0 copy-start.3
  0.0 0.0 copy-start.4
  0.0 0.0 copy-start.5
  0.0 0.0 copy-start.6
  0.0 4.3 %chunk.1 = (f32[8,160,128]{2,1,0:T(8,128)}, f32[6,128,128]{2,1,0:T(8,128)}) custom-call(bf16[3,128,128]{2,1,0:T(8,128)(2,1)} %proj_ref.1, bf16[128,128]{1,0:T(8,128)(2,1)} %grad_ref.1, f32[2,1,128]{2,1,0:T(1,128)} %logit_ref.1, f32[1,2]{1,0:T(1,128)} %bitcast.4), custom_call_target="tpu_custom_call" | custom-call | tf_op jit(solution)/shard_map/chunk/pallas_call | solution.py:375
  4.3 0.0 copy-start.2
  4.3 25.2 %all_to_all.15.in_ref = f32[8,160,128]{2,1,0:T(8,128)S(1)} all-to-all(f32[8,160,128]{2,1,0:T(8,128)} %get-tuple-element.13), channel_id=1, replica_groups=mesh['x'=4,'y'=8,'z'=8,'c'=2] {'y'}, dimensions={0} | all-to-all | bytes 1310720 | tf_op jit(solution)/shard_map/all_to_all | solution.py:412
  29.6 1.2 %row.1 = (f32[32,32,128]{2,1,0:T(8,128)S(1)}, f32[2,128,128]{2,1,0:T(8,128)S(1)}) custom-call(f32[8,160,128]{2,1,0:T(8,128)S(1)} %all_to_all.15.in_ref), custom_call_target="tpu_custom_call" | custom-call | tf_op jit(solution)/shard_map/row/pallas_call | solution.py:375
  30.7 20.1 %all_to_all.16.in_ref = f32[32,32,128]{2,1,0:T(8,128)S(1)} all-to-all(f32[32,32,128]{2,1,0:T(8,128)S(1)} %get-tuple-element.15), channel_id=1, replica_groups={{112,240,368,496,96,224,352,480,80,208,336,464,64,192,320,448,48,176,30..., dimensions={0} | all-to-all | bytes 1048576 | tf_op jit(solution)/shard_map/all_to_all | solution.py:421
  50.8 0.0 copy-done
  50.8 0.0 copy-done.1
  50.8 0.0 copy-done.3
  50.8 0.0 copy-done.4
  50.8 0.0 copy-done.5
  50.8 0.0 copy-done.6
  50.8 0.0 copy-done.2
  50.8 1.8 %grad.1 = (f32[8,128,128]{2,1,0:T(8,128)S(1)}, bf16[3,128,128]{2,1,0:T(8,128)(2,1)S(1)}, f32[128,128]{1,0:T(8,128)S(1)}) custom-call(bf16[3,128,128]{2,1,0:T(8,128)(2,1)S(1)} %copy-done.1, bf16[128,128]{1,0:T(8,128)(2,1)S(1)} %copy-done.3, f32[2,1,128]{2,1,0:T(1,128)S(1)} %copy-done.5, f32[1,2]{1,0:T(1,128)S(1)} %bitcast.5, ...), custom_call_target="tpu_custom_call" | custom-call | tf_op jit(solution)/shard_map/grad/pallas_call | solution.py:375
  52.6 6.3 %collective-permute-start = (f32[8,128,128]{2,1,0:T(8,128)S(1)}, f32[8,128,128]{2,1,0:T(8,128)S(1)}, u32[]{:S(2)}, u32[]{:S(2)}) collective-permute-start(f32[8,128,128]{2,1,0:T(8,128)S(1)} %get-tuple-element.18), channel_id=1, source_target_pairs={{0,1},{1,0},{2,3},{3,2},{4,5},{5,4},{6,7},{7,6},{8,9},{9,8},{10,11... | collective-permute-start | bytes 1572872 | tf_op jit(solution)/shard_map/ppermute | solution.py:443
  59.0 1.5 %collective-permute-done.other_ref = f32[8,128,128]{2,1,0:T(8,128)S(1)} collective-permute-done((f32[8,128,128]{2,1,0:T(8,128)S(1)}, f32[8,128,128]{2,1,0:T(8,128)S(1)}, u32[]{:S(2)}, u32[]{:S(2)}) %collective-permute-start) | collective-permute-done | bytes 524320 | tf_op jit(solution)/shard_map/ppermute | solution.py:443
  60.5 0.5 keep.1
  61.0 23.8 %all_to_all.17 = f32[8,128,128]{2,1,0:T(8,128)S(1)} all-to-all(f32[8,128,128]{2,1,0:T(8,128)S(1)} %keep.1), channel_id=1, replica_groups={{14,10,6,12,8,4,2,0},{15,11,7,13,9,5,3,1},{30,26,22,28,24,20,18,16},{31..., dimensions={0} | all-to-all | bytes 1048576 | tf_op jit(solution)/shard_map/all_to_all | solution.py:455
  84.8 0.6 reduce_sum.9
Async XLA Ops:
  0.0 50.8 %copy-start = (bf16[3,2048,128]{2,1,0:T(8,128)(2,1)S(1)}, bf16[3,2048,128]{2,1,0:T(8,128)(2,1)}, u32[]{:S(2)}) copy-start(bf16[3,2048,128]{2,1,0:T(8,128)(2,1)} %weight_ref.3) | copy-start | bytes 4718596
  0.0 50.8 %copy-start.1 = (bf16[3,128,128]{2,1,0:T(8,128)(2,1)S(1)}, bf16[3,128,128]{2,1,0:T(8,128)(2,1)}, u32[]{:S(2)}) copy-start(bf16[3,128,128]{2,1,0:T(8,128)(2,1)} %proj_ref.1) | copy-start | bytes 294916
  0.0 50.8 %copy-start.3 = (bf16[128,128]{1,0:T(8,128)(2,1)S(1)}, bf16[128,128]{1,0:T(8,128)(2,1)}, u32[]{:S(2)}) copy-start(bf16[128,128]{1,0:T(8,128)(2,1)} %grad_ref.1) | copy-start | bytes 98308
  0.0 50.8 %copy-start.4 = (bf16[2,1,2048]{2,0,1:T(2,128)(2,1)S(1)}, bf16[2,1,2048]{2,0,1:T(2,128)(2,1)}, u32[]{:S(2)}) copy-start(bf16[2,1,2048]{2,0,1:T(2,128)(2,1)} %param.11) | copy-start | bytes 24580
  0.0 50.8 %copy-start.5 = (f32[2,1,128]{2,1,0:T(1,128)S(1)}, f32[2,1,128]{2,1,0:T(1,128)}, u32[]{:S(2)}) copy-start(f32[2,1,128]{2,1,0:T(1,128)} %logit_ref.1) | copy-start | bytes 3076
  0.0 50.8 %copy-start.6 = (f32[2,1]{0,1:T(1,128)S(1)}, f32[2,1]{0,1:T(1,128)}, u32[]{:S(2)}) copy-start(f32[2,1]{0,1:T(1,128)} %param.9) | copy-start | bytes 28
  4.3 46.5 %copy-start.2 = (f32[6,128,128]{2,1,0:T(8,128)S(1)}, f32[6,128,128]{2,1,0:T(8,128)}, u32[]{:S(2)}) copy-start(f32[6,128,128]{2,1,0:T(8,128)} %get-tuple-element.12.saved_ref) | copy-start | bytes 1179652
  52.6 7.9 %collective-permute-start = (f32[8,128,128]{2,1,0:T(8,128)S(1)}, f32[8,128,128]{2,1,0:T(8,128)S(1)}, u32[]{:S(2)}, u32[]{:S(2)}) collective-permute-start(f32[8,128,128]{2,1,0:T(8,128)S(1)} %get-tuple-element.18), channel_id=1, source_target_pairs={{0,1},{1,0},{2,3},{3,2},{4,5},{5,4},{6,7},{7,6},{8,9},{9,8},{10,11... | collective-permute-start | bytes 1572872 | tf_op jit(solution)/shard_map/ppermute | solution.py:443

commit v4 on v3

--- a/solution.py
+++ b/solution.py
@@ -15,7 +15,6 @@
 GRID_ORDER = tuple(x * COLS + y for y in reversed(range(COLS)) for x in range(ROWS))
 SCALE = DK ** (-0.5)
 F32 = jnp.float32
-CHUNK_LIMIT = 60 << 20
 
 NN = (((1,), (0,)), ((), ()))
 NT = (((1,), (1,)), ((), ()))
@@ -66,16 +65,16 @@
     return raw * scale, scale
 
 
-def gates(logit_ref, head_ref, row, col):
-    heads = head_ref[...]
-    rate = jnp.exp(heads[:, 0:1])
-    shifted = logit_ref[0] + heads[:, 1:2]
+def gates(gate_rows_ref, row, col):
+    rows = gate_rows_ref[...]
+    rate = jnp.exp(rows[2:3, 0:1])
+    shifted = rows[0:1] + rows[2:3, 1:2]
     soft = jnp.maximum(shifted, 0.0) + jnp.log1p(jnp.exp(-jnp.abs(shifted)))
     decay_row = -rate * soft
     cumul = lane_sum(jnp.where(col <= row, decay_row, 0.0))
     cumul_row = jnp.sum(jnp.where(row == col, cumul, 0.0), axis=0, keepdims=True)
     last = cumul_row[:, TOK - 1 :]
-    write = lane_sum(jnp.where(row == col, jax.nn.sigmoid(logit_ref[1]), 0.0))
+    write = lane_sum(jnp.where(row == col, jax.nn.sigmoid(rows[1:2]), 0.0))
     lower = row >= col
     ratio = jnp.where(lower, jnp.exp(jnp.where(lower, cumul - cumul_row, 0.0)), 0.0)
     slope = lane_sum(jnp.where(row == col, -rate * jax.nn.sigmoid(shifted), 0.0))
@@ -102,50 +101,17 @@
 
 
 def chunk_kernel(
-    proj_hbm,
-    grad_hbm,
-    logit_hbm,
-    head_hbm,
-    out_hbm,
-    saved_hbm,
     proj_ref,
-    grad_ref,
-    logit_ref,
-    head_ref,
-    step_ref,
-    edge_ref,
+    gate_rows_ref,
+    out_ref,
     saved_ref,
-    in_sems,
-    out_sems,
 ):
-    pairs = (
-        (logit_hbm, logit_ref),
-        (head_hbm, head_ref),
-        (proj_hbm, proj_ref),
-        (grad_hbm, grad_ref),
-    )
-    copies = [pltpu.make_async_copy(*pair, in_sems.at[i]) for i, pair in enumerate(pairs)]
-    for copy in copies:
-        copy.start()
-    for copy in copies:
-        copy.wait()
-    leaving = []
-
-    def leave(source, target):
-        copy = pltpu.make_async_copy(source, target, out_sems.at[len(leaving)])
-        copy.start()
-        leaving.append(copy)
-
-    def save(at, value):
-        saved_ref[at] = value
-        leave(saved_ref.at[at], saved_hbm.at[at])
-
     row, col = iotas()
-    grown, rest, total, write, ratio, _ = gates(logit_ref, head_ref, row, col)
+    grown, rest, total, write, ratio, _ = gates(gate_rows_ref, row, col)
     queries = unit(proj_ref[0].astype(F32))[0] * SCALE
     keys = unit(proj_ref[1].astype(F32))[0]
     values = proj_ref[2].astype(F32)
-    out_grad = grad_ref[...].astype(F32)
+    out_grad = proj_ref[3].astype(F32)
     inner = dot(jnp.concatenate([keys, queries], 0), keys, NT)
     bare = jnp.where(row > col, ratio * inner[:TOK], 0.0)
     attend = ratio * inner[TOK:]
@@ -157,22 +123,18 @@
     rest_keys = rest * keys
     moved = dot(solved, rest_keys, TN)
     eye = jnp.where(row == col, 1.0, 0.0).astype(F32)
-    step_ref[...] = total * eye - moved[:DK]
-    for peer in range(COLS):
-        leave(step_ref, out_hbm.at[peer, pl.ds(0, DK)])
+    step = total * eye - moved[:DK]
     back = direct - dot(attended, key_weights, TN)
     for peer in range(COLS):
-        edge_ref[peer, :SLICE] = moved[DK + peer * SLICE : DK + (peer + 1) * SLICE]
-        edge_ref[peer, SLICE:] = back[peer * SLICE : (peer + 1) * SLICE]
-    leave(edge_ref, out_hbm.at[:, pl.ds(DK, 2 * SLICE)])
-    save(0, inverse.T)
-    save(1, key_weights)
-    save(2, base)
-    save(3, attend)
-    save(4, bare)
-    save(5, attended)
-    for copy in leaving:
-        copy.wait()
+        out_ref[peer, :DK] = step
+        out_ref[peer, DK : DK + SLICE] = moved[DK + peer * SLICE : DK + (peer + 1) * SLICE]
+        out_ref[peer, DK + SLICE :] = back[peer * SLICE : (peer + 1) * SLICE]
+    saved_ref[0] = inverse.T
+    saved_ref[1] = key_weights
+    saved_ref[2] = base
+    saved_ref[3] = attend
+    saved_ref[4] = bare
+    saved_ref[5] = attended
 
 
 def row_kernel(in_ref, out_ref, own_ref, scratch_ref):
@@ -248,9 +210,7 @@
 
 def grad_kernel(
     proj_ref,
-    grad_ref,
-    logit_ref,
-    head_ref,
+    gate_rows_ref,
     weight_ref,
     gate_ref,
     saved_ref,
@@ -282,12 +242,12 @@
     later = halves(dot(g_row, own_ref[1], NT) + part(here_x, 1))
 
     row, col = iotas()
-    grown, rest, total, write, ratio, slope = gates(logit_ref, head_ref, row, col)
+    grown, rest, total, write, ratio, slope = gates(gate_rows_ref, row, col)
     q_unit, q_scale = unit(proj_ref[0].astype(F32))
     queries = q_unit * SCALE
     keys, k_scale = unit(proj_ref[1].astype(F32))
     values = proj_ref[2].astype(F32)
-    out_grad = grad_ref[...].astype(F32)
+    out_grad = proj_ref[3].astype(F32)
     rest_keys = rest * keys
     attend = saved_ref[3]
     bare = saved_ref[4]
@@ -364,50 +324,36 @@
 
 
 VMEM = pl.BlockSpec(memory_space=pltpu.VMEM)
-HBM = pl.BlockSpec(memory_space=pltpu.HBM)
 
 
 def like(*shape):
     return jax.ShapeDtypeStruct(shape, F32)
 
 
-def call(kernel, name, out_shape, in_specs, *args, scratch=(), limit=16 << 20, space=VMEM):
+def call(kernel, name, out_shape, in_specs, *args, scratch=()):
     return pl.pallas_call(
         kernel,
         out_shape=out_shape,
         in_specs=in_specs,
-        out_specs=jax.tree.map(lambda _: space, out_shape),
+        out_specs=jax.tree.map(lambda _: VMEM, out_shape),
         scratch_shapes=scratch,
-        compiler_params=pltpu.CompilerParams(vmem_limit_bytes=limit),
+        compiler_params=pltpu.CompilerParams(vmem_limit_bytes=16 << 20),
         name=name,
     )(*args)
 
 
 def shards(projected, out_grad, logits, head_params, qkv_weight, gate_weight):
-    heads = head_params.T
+    packed = jnp.concatenate([projected, out_grad[None]], 0)
+    padded = jnp.pad(head_params.T, ((0, 0), (0, TOK - 2)))
+    gate_rows = jnp.concatenate([logits[:, 0], padded], 0)
     gate = jnp.transpose(gate_weight, (1, 0, 2))[0]
     chunks, saved = call(
         chunk_kernel,
         "chunk",
         (like(COLS, DK + 2 * SLICE, DK), like(6, DK, DK)),
-        [HBM] * 4,
-        projected,
-        out_grad,
-        logits,
-        heads,
-        scratch=[
-            pltpu.VMEM((3, TOK, DK), BF16),
-            pltpu.VMEM((TOK, DK), BF16),
-            pltpu.VMEM((2, 1, TOK), F32),
-            pltpu.VMEM((1, 2), F32),
-            pltpu.VMEM((DK, DK), F32),
-            pltpu.VMEM((COLS, 2 * SLICE, DK), F32),
-            pltpu.VMEM((6, DK, DK), F32),
-            pltpu.SemaphoreType.DMA((4,)),
-            pltpu.SemaphoreType.DMA((COLS + 7,)),
-        ],
-        space=HBM,
-        limit=CHUNK_LIMIT,
+        [VMEM] * 2,
+        packed,
+        gate_rows,
     )
     chunks = lax.all_to_all(chunks, "y", 0, 0, tiled=True)
     rows, own = call(
@@ -429,11 +375,9 @@
             jax.ShapeDtypeStruct((3, TOK, DK), BF16),
             like(TOK, DK),
         ),
-        [VMEM] * 9,
-        projected,
-        out_grad,
-        logits,
-        heads,
+        [VMEM] * 7,
+        packed,
+        gate_rows,
         qkv_weight,
         gate,
         saved,

time: 86.3 us -> 85.4 us (0.990)
  Pallas kernels: 7.68 us -> 5.55 us
  other arithmetic: 0.64 us -> 2.27 us
    pallas_call x4, Pallas kernels: 7.68 us -> 5.55 us  [call(): pl.pallas_call(kernel, out_shape=out_shape, in_specs=in_specs, out_specs=...]
    concatenate x0 -> x2, other arithmetic: none -> 1.63 us  [the longest x1 0.93 us: shards(): packed = jnp.concatenate([projected, out_grad[None]], 0)]
where the time goes in v4:
time: 85.4 us; the launch traced here: 84.5 us
  blocking collectives  68.7 us (80%)
  starting transfers between devices  6.34 us (7%)
  Pallas kernels  5.55 us (6%)
  other arithmetic  2.27 us (3%)
  waiting for transfers between devices  1.51 us (2%)
    all_to_all x1, blocking collectives, shards(): chunks = lax.all_to_all(chunks, 'y', 0, 0, tiled=True)  25.5 us
    all_to_all x1, blocking collectives, shards(): lax.all_to_all(part, 'z', 0, 0, tiled=True, axis_index_groups=[list(ORDER)])  23.8 us
    all_to_all x1, blocking collectives, shards(): lax.all_to_all(rows, ('x', 'y'), 0, 0, tiled=True, axis_index_groups=[lis...  19.4 us
    ppermute x1, starting transfers between devices, shards(): other = lax.ppermute(send, 'c', [(0, 1), (1, 0)])  6.34 us
    pallas_call x4, Pallas kernels, call(): pl.pallas_call(kernel, out_shape=out_shape, in_specs=in_specs, out_specs=...  5.55 us
  transfers between devices with their start and end apart: 1, of which 1 were waited for; matrix products, arithmetic and copies ran while one was open for 0% of the time, Pallas kernels for 0%

profile of v4, /device:TPU:1, one launch (start us, length us, event | category | flops | bytes accessed | tf_op | source)
XLA Modules:
  0.0 84.5 jit_solution(4796564688922584212)
XLA Ops:
  0.0 0.7 select_maximum_fusion.gate_rows_ref
  0.7 0.9 %pad_maximum_fusion.proj_ref = bf16[4,128,128]{2,1,0:T(8,128)(2,1)S(1)} fusion(bf16[1,128,128]{2,1,0:T(8,128)(2,1)} %bitcast.6, bf16[3,128,128]{2,1,0:T(8,128)(2,1)} %param.6), kind=kLoop, calls=%fused_computation | loop fusion | flops 65536 | bytes 262144 | tf_op jit(solution)/shard_map/concatenate | solution.py:346
  1.6 0.0 copy-start
  1.6 0.0 copy-start.1
  1.7 2.1 %chunk.1 = (f32[8,160,128]{2,1,0:T(8,128)S(1)}, f32[6,128,128]{2,1,0:T(8,128)S(1)}) custom-call(bf16[4,128,128]{2,1,0:T(8,128)(2,1)S(1)} %pad_maximum_fusion.proj_ref, f32[3,128]{1,0:T(4,128)S(1)} %select_maximum_fusion.gate_rows_ref), custom_call_target="tpu_custom_call" | custom-call | tf_op jit(solution)/shard_map/chunk/pallas_call | solution.py:334
  3.8 25.5 %all_to_all.15.in_ref = f32[8,160,128]{2,1,0:T(8,128)S(1)} all-to-all(f32[8,160,128]{2,1,0:T(8,128)S(1)} %get-tuple-element.13), channel_id=1, replica_groups=mesh['x'=4,'y'=8,'z'=8,'c'=2] {'y'}, dimensions={0} | all-to-all | bytes 1310720 | tf_op jit(solution)/shard_map/all_to_all | solution.py:358
  29.3 1.1 %row.1 = (f32[32,32,128]{2,1,0:T(8,128)S(1)}, f32[2,128,128]{2,1,0:T(8,128)S(1)}) custom-call(f32[8,160,128]{2,1,0:T(8,128)S(1)} %all_to_all.15.in_ref), custom_call_target="tpu_custom_call" | custom-call | tf_op jit(solution)/shard_map/row/pallas_call | solution.py:334
  30.5 19.4 %all_to_all.16.in_ref = f32[32,32,128]{2,1,0:T(8,128)S(1)} all-to-all(f32[32,32,128]{2,1,0:T(8,128)S(1)} %get-tuple-element.15), channel_id=1, replica_groups={{112,240,368,496,96,224,352,480,80,208,336,464,64,192,320,448,48,176,30..., dimensions={0} | all-to-all | bytes 1048576 | tf_op jit(solution)/shard_map/all_to_all | solution.py:367
  49.9 0.0 copy-done
  49.9 0.0 copy-done.1
  49.9 1.8 %grad.1 = (f32[8,128,128]{2,1,0:T(8,128)S(1)}, bf16[3,128,128]{2,1,0:T(8,128)(2,1)S(1)}, f32[128,128]{1,0:T(8,128)S(1)}) custom-call(bf16[4,128,128]{2,1,0:T(8,128)(2,1)S(1)} %pad_maximum_fusion.proj_ref, f32[3,128]{1,0:T(4,128)S(1)} %select_maximum_fusion.gate_rows_ref, bf16[3,2048,128]{2,1,0:T(8,128)(2,1)S(1)} %copy-done, bf16[2,2048]{1,0:T(2,128)(2,1)S(1)} %bitcast.4, ...), custom_call_target="tpu_custom_call" | custom-call | tf_op jit(solution)/shard_map/grad/pallas_call | solution.py:334
  51.7 6.3 %collective-permute-start = (f32[8,128,128]{2,1,0:T(8,128)S(1)}, f32[8,128,128]{2,1,0:T(8,128)S(1)}, u32[]{:S(2)}, u32[]{:S(2)}) collective-permute-start(f32[8,128,128]{2,1,0:T(8,128)S(1)} %get-tuple-element.18), channel_id=1, source_target_pairs={{0,1},{1,0},{2,3},{3,2},{4,5},{5,4},{6,7},{7,6},{8,9},{9,8},{10,11... | collective-permute-start | bytes 1572872 | tf_op jit(solution)/shard_map/ppermute | solution.py:387
  58.1 1.5 %collective-permute-done.other_ref = f32[8,128,128]{2,1,0:T(8,128)S(1)} collective-permute-done((f32[8,128,128]{2,1,0:T(8,128)S(1)}, f32[8,128,128]{2,1,0:T(8,128)S(1)}, u32[]{:S(2)}, u32[]{:S(2)}) %collective-permute-start) | collective-permute-done | bytes 524320 | tf_op jit(solution)/shard_map/ppermute | solution.py:387
  59.6 0.5 keep.1
  60.1 23.8 %all_to_all.17 = f32[8,128,128]{2,1,0:T(8,128)S(1)} all-to-all(f32[8,128,128]{2,1,0:T(8,128)S(1)} %keep.1), channel_id=1, replica_groups={{14,10,6,12,8,4,2,0},{15,11,7,13,9,5,3,1},{30,26,22,28,24,20,18,16},{31..., dimensions={0} | all-to-all | bytes 1048576 | tf_op jit(solution)/shard_map/all_to_all | solution.py:399
  83.8 0.6 reduce_sum.9
Async XLA Ops:
  1.6 48.3 %copy-start = (bf16[3,2048,128]{2,1,0:T(8,128)(2,1)S(1)}, bf16[3,2048,128]{2,1,0:T(8,128)(2,1)}, u32[]{:S(2)}) copy-start(bf16[3,2048,128]{2,1,0:T(8,128)(2,1)} %weight_ref.3) | copy-start | bytes 4718596
  1.6 48.3 %copy-start.1 = (bf16[2,1,2048]{2,0,1:T(2,128)(2,1)S(1)}, bf16[2,1,2048]{2,0,1:T(2,128)(2,1)}, u32[]{:S(2)}) copy-start(bf16[2,1,2048]{2,0,1:T(2,128)(2,1)} %param.11) | copy-start | bytes 24580
  51.7 7.9 %collective-permute-start = (f32[8,128,128]{2,1,0:T(8,128)S(1)}, f32[8,128,128]{2,1,0:T(8,128)S(1)}, u32[]{:S(2)}, u32[]{:S(2)}) collective-permute-start(f32[8,128,128]{2,1,0:T(8,128)S(1)} %get-tuple-element.18), channel_id=1, source_target_pairs={{0,1},{1,0},{2,3},{3,2},{4,5},{5,4},{6,7},{7,6},{8,9},{9,8},{10,11... | collective-permute-start | bytes 1572872 | tf_op jit(solution)/shard_map/ppermute | solution.py:387

commit v5 on v4

--- a/solution.py
+++ b/solution.py
@@ -81,7 +81,7 @@
     return jnp.exp(cumul), jnp.exp(last - cumul), jnp.exp(last), write, ratio, slope
 
 
-def inverse_of(strict, row, col):
+def inverse_of(strict, given, row, col):
     eye = jnp.where(row == col, 1.0, 0.0).astype(F32)
 
     def same(level):
@@ -89,15 +89,18 @@
 
     out = eye - jnp.where(same(1), strict, 0.0)
     for low, high in ((1, 4), (4, 7)):
-        near = halves(out)
         off = jnp.where(same(high) & ~same(low), strict, 0.0)
-        power = dot(near, off)
+        if high == 7:
+            first = dot(out, jnp.concatenate([off, given], 1))
+            power, out = first[:, :TOK], jnp.concatenate([out, first[:, TOK:]], 1)
+        else:
+            power = dot(out, off)
         both = dot(power, jnp.concatenate([power, out], 1))
         power, out = both[:, :TOK], out - both[:, TOK:]
         both = dot(power, jnp.concatenate([power, out], 1))
         power, out = both[:, :TOK], out + both[:, TOK:]
         out = out + dot(power, out)
-    return out
+    return out[:, :TOK], out[:, TOK:]
 
 
 def chunk_kernel(
@@ -115,10 +118,10 @@
     inner = dot(jnp.concatenate([keys, queries], 0), keys, NT)
     bare = jnp.where(row > col, ratio * inner[:TOK], 0.0)
     attend = ratio * inner[TOK:]
-    inverse = inverse_of(bare * write, row, col)
+    given = jnp.concatenate([(write * grown) * keys, write * values], 1)
+    inverse, solved = inverse_of(bare * write, given, row, col)
     attended = dot(attend, out_grad, TN)
     direct = dot(out_grad, grown * queries, TN)
-    solved = dot(inverse, jnp.concatenate([(write * grown) * keys, write * values], 1))
     key_weights, base = solved[:, :DK], solved[:, DK:]
     rest_keys = rest * keys
     moved = dot(solved, rest_keys, TN)
@@ -314,13 +317,12 @@
     return acc
 
 
-def keep_kernel(low_ref, slope_ref, weight_ref, gate_ref, other_ref, out_ref):
+def keep_kernel(low_ref, slope_ref, weight_ref, gate_ref, out_ref):
     here_c = lax.axis_index("c")
     low = [low_ref[source] for source in range(3)]
     slopes = (slope_ref[:, 0:1], slope_ref[:, 1:2])
     for slot, peer in enumerate(ORDER):
-        own = projected_to(2 * peer + here_c, low, slopes, weight_ref, gate_ref)
-        out_ref[slot] = other_ref[slot] + own
+        out_ref[slot] = projected_to(2 * peer + here_c, low, slopes, weight_ref, gate_ref)
 
 
 VMEM = pl.BlockSpec(memory_space=pltpu.VMEM)
@@ -389,13 +391,13 @@
         keep_kernel,
         "keep",
         like(COLS, TOK, DK),
-        [VMEM] * 5,
+        [VMEM] * 4,
         low,
         slopes,
         qkv_weight,
         gate,
-        other,
-    )
+    )
+    part = part + other
     summed = lax.all_to_all(
         part, "z", 0, 0, tiled=True, axis_index_groups=[list(ORDER)]
     )

time: 85.4 us -> 84.9 us (level)
  transfers between devices with their start and end apart: 1 -> 1, of which waited for: 1 -> 1; matrix products, arithmetic and copies ran while one was open for 0% -> 0% of each run, Pallas kernels for 0% -> 1%
where the time goes in v5:
time: 84.9 us; the launch traced here: 84 us
  blocking collectives  68.8 us (81%)
  starting transfers between devices  6.35 us (7%)
  Pallas kernels  5.49 us (6%)
  other arithmetic  2.34 us (3%)
  waiting for transfers between devices  1.03 us (1%)
    all_to_all x1, blocking collectives, shards(): chunks = lax.all_to_all(chunks, 'y', 0, 0, tiled=True)  25.5 us
    all_to_all x1, blocking collectives, shards(): lax.all_to_all(part, 'z', 0, 0, tiled=True, axis_index_groups=[list(ORDER)])  23.8 us
    all_to_all x1, blocking collectives, shards(): lax.all_to_all(rows, ('x', 'y'), 0, 0, tiled=True, axis_index_groups=[lis...  19.4 us
    ppermute x1, starting transfers between devices, shards(): other = lax.ppermute(send, 'c', [(0, 1), (1, 0)])  6.35 us
    pallas_call x4, Pallas kernels, call(): pl.pallas_call(kernel, out_shape=out_shape, in_specs=in_specs, out_specs=...  5.49 us
  transfers between devices with their start and end apart: 1, of which 1 were waited for; matrix products, arithmetic and copies ran while one was open for 0% of the time, Pallas kernels for 1%

profile of v5, /device:TPU:1, one launch (start us, length us, event | category | flops | bytes accessed | tf_op | source)
XLA Modules:
  0.0 84.0 jit_solution(12089138170944985419)
XLA Ops:
  0.0 0.7 select_maximum_fusion.gate_rows_ref
  0.7 0.9 %pad_maximum_fusion.proj_ref = bf16[4,128,128]{2,1,0:T(8,128)(2,1)S(1)} fusion(bf16[1,128,128]{2,1,0:T(8,128)(2,1)} %bitcast.6, bf16[3,128,128]{2,1,0:T(8,128)(2,1)} %param.6), kind=kLoop, calls=%fused_computation | loop fusion | flops 65536 | bytes 262144 | tf_op jit(solution)/shard_map/concatenate | solution.py:348
  1.6 0.0 copy-start
  1.6 0.0 copy-start.1
  1.7 2.1 %chunk.1 = (f32[8,160,128]{2,1,0:T(8,128)S(1)}, f32[6,128,128]{2,1,0:T(8,128)S(1)}) custom-call(bf16[4,128,128]{2,1,0:T(8,128)(2,1)S(1)} %pad_maximum_fusion.proj_ref, f32[3,128]{1,0:T(4,128)S(1)} %select_maximum_fusion.gate_rows_ref), custom_call_target="tpu_custom_call" | custom-call | tf_op jit(solution)/shard_map/chunk/pallas_call | solution.py:336
  3.7 25.5 %all_to_all.15.in_ref = f32[8,160,128]{2,1,0:T(8,128)S(1)} all-to-all(f32[8,160,128]{2,1,0:T(8,128)S(1)} %get-tuple-element.13), channel_id=1, replica_groups=mesh['x'=4,'y'=8,'z'=8,'c'=2] {'y'}, dimensions={0} | all-to-all | bytes 1310720 | tf_op jit(solution)/shard_map/all_to_all | solution.py:360
  29.3 1.1 %row.1 = (f32[32,32,128]{2,1,0:T(8,128)S(1)}, f32[2,128,128]{2,1,0:T(8,128)S(1)}) custom-call(f32[8,160,128]{2,1,0:T(8,128)S(1)} %all_to_all.15.in_ref), custom_call_target="tpu_custom_call" | custom-call | tf_op jit(solution)/shard_map/row/pallas_call | solution.py:336
  30.4 19.4 %all_to_all.16.in_ref = f32[32,32,128]{2,1,0:T(8,128)S(1)} all-to-all(f32[32,32,128]{2,1,0:T(8,128)S(1)} %get-tuple-element.15), channel_id=1, replica_groups={{112,240,368,496,96,224,352,480,80,208,336,464,64,192,320,448,48,176,30..., dimensions={0} | all-to-all | bytes 1048576 | tf_op jit(solution)/shard_map/all_to_all | solution.py:369
  49.8 0.0 copy-done
  49.8 0.0 copy-done.1
  49.8 1.8 %grad.1 = (f32[8,128,128]{2,1,0:T(8,128)S(1)}, bf16[3,128,128]{2,1,0:T(8,128)(2,1)S(1)}, f32[128,128]{1,0:T(8,128)S(1)}) custom-call(bf16[4,128,128]{2,1,0:T(8,128)(2,1)S(1)} %pad_maximum_fusion.proj_ref, f32[3,128]{1,0:T(4,128)S(1)} %select_maximum_fusion.gate_rows_ref, bf16[3,2048,128]{2,1,0:T(8,128)(2,1)S(1)} %copy-done, bf16[2,2048]{1,0:T(2,128)(2,1)S(1)} %bitcast.4, ...), custom_call_target="tpu_custom_call" | custom-call | tf_op jit(solution)/shard_map/grad/pallas_call | solution.py:336
  51.6 6.3 %collective-permute-start = (f32[8,128,128]{2,1,0:T(8,128)S(1)}, f32[8,128,128]{2,1,0:T(8,128)S(1)}, u32[]{:S(2)}, u32[]{:S(2)}) collective-permute-start(f32[8,128,128]{2,1,0:T(8,128)S(1)} %get-tuple-element.18), channel_id=1, source_target_pairs={{0,1},{1,0},{2,3},{3,2},{4,5},{5,4},{6,7},{7,6},{8,9},{9,8},{10,11... | collective-permute-start | bytes 1572872 | tf_op jit(solution)/shard_map/ppermute | solution.py:389
  58.0 0.5 keep.1
  58.5 1.0 %collective-permute-done = f32[8,128,128]{2,1,0:T(8,128)S(1)} collective-permute-done((f32[8,128,128]{2,1,0:T(8,128)S(1)}, f32[8,128,128]{2,1,0:T(8,128)S(1)}, u32[]{:S(2)}, u32[]{:S(2)}) %collective-permute-start) | collective-permute-done | bytes 524320 | tf_op jit(solution)/shard_map/ppermute | solution.py:389
  59.5 0.1 add.5
  59.6 23.8 %all_to_all.17 = f32[8,128,128]{2,1,0:T(8,128)S(1)} all-to-all(f32[8,128,128]{2,1,0:T(8,128)S(1)} %add.5), channel_id=1, replica_groups={{14,10,6,12,8,4,2,0},{15,11,7,13,9,5,3,1},{30,26,22,28,24,20,18,16},{31..., dimensions={0} | all-to-all | bytes 1048576 | tf_op jit(solution)/shard_map/all_to_all | solution.py:401
  83.4 0.6 reduce_sum.9
Async XLA Ops:
  1.6 48.2 %copy-start = (bf16[3,2048,128]{2,1,0:T(8,128)(2,1)S(1)}, bf16[3,2048,128]{2,1,0:T(8,128)(2,1)}, u32[]{:S(2)}) copy-start(bf16[3,2048,128]{2,1,0:T(8,128)(2,1)} %weight_ref.3) | copy-start | bytes 4718596
  1.6 48.2 %copy-start.1 = (bf16[2,1,2048]{2,0,1:T(2,128)(2,1)S(1)}, bf16[2,1,2048]{2,0,1:T(2,128)(2,1)}, u32[]{:S(2)}) copy-start(bf16[2,1,2048]{2,0,1:T(2,128)(2,1)} %param.11) | copy-start | bytes 24580
  51.6 7.9 %collective-permute-start = (f32[8,128,128]{2,1,0:T(8,128)S(1)}, f32[8,128,128]{2,1,0:T(8,128)S(1)}, u32[]{:S(2)}, u32[]{:S(2)}) collective-permute-start(f32[8,128,128]{2,1,0:T(8,128)S(1)} %get-tuple-element.18), channel_id=1, source_target_pairs={{0,1},{1,0},{2,3},{3,2},{4,5},{5,4},{6,7},{7,6},{8,9},{9,8},{10,11... | collective-permute-start | bytes 1572872 | tf_op jit(solution)/shard_map/ppermute | solution.py:389

commit v6 on v5

--- a/solution.py
+++ b/solution.py
@@ -11,7 +11,7 @@
 ROWS = 4
 COLS = 8
 SLICE = DK // COLS
-ORDER = (7, 5, 3, 6, 4, 2, 1, 0)
+ORDER = (7, 6, 5, 4, 3, 2, 1, 0)
 GRID_ORDER = tuple(x * COLS + y for y in reversed(range(COLS)) for x in range(ROWS))
 SCALE = DK ** (-0.5)
 F32 = jnp.float32

time: 84.9 us -> 84.3 us (level)
  blocking collectives: 68.8 us -> 67.9 us
where the time goes in v6:
time: 84.3 us; the launch traced here: 83.2 us
  blocking collectives  67.9 us (81%)
  starting transfers between devices  6.35 us (8%)
  Pallas kernels  5.49 us (7%)
  other arithmetic  2.34 us (3%)
  waiting for transfers between devices  1.03 us (1%)
    all_to_all x1, blocking collectives, shards(): chunks = lax.all_to_all(chunks, 'y', 0, 0, tiled=True)  25.5 us
    all_to_all x1, blocking collectives, shards(): lax.all_to_all(part, 'z', 0, 0, tiled=True, axis_index_groups=[list(ORDER)])  23 us
    all_to_all x1, blocking collectives, shards(): lax.all_to_all(rows, ('x', 'y'), 0, 0, tiled=True, axis_index_groups=[lis...  19.4 us
    ppermute x1, starting transfers between devices, shards(): other = lax.ppermute(send, 'c', [(0, 1), (1, 0)])  6.35 us
    pallas_call x4, Pallas kernels, call(): pl.pallas_call(kernel, out_shape=out_shape, in_specs=in_specs, out_specs=...  5.49 us
  transfers between devices with their start and end apart: 1, of which 1 were waited for; matrix products, arithmetic and copies ran while one was open for 0% of the time, Pallas kernels for 1%

profile of v6, /device:TPU:1, one launch (start us, length us, event | category | flops | bytes accessed | tf_op | source)
XLA Modules:
  0.0 83.2 jit_solution(13694942700978098866)
XLA Ops:
  0.0 0.7 select_maximum_fusion.gate_rows_ref
  0.7 0.9 %pad_maximum_fusion.proj_ref = bf16[4,128,128]{2,1,0:T(8,128)(2,1)S(1)} fusion(bf16[1,128,128]{2,1,0:T(8,128)(2,1)} %bitcast.6, bf16[3,128,128]{2,1,0:T(8,128)(2,1)} %param.6), kind=kLoop, calls=%fused_computation | loop fusion | flops 65536 | bytes 262144 | tf_op jit(solution)/shard_map/concatenate | solution.py:348
  1.6 0.0 copy-start
  1.6 0.0 copy-start.1
  1.7 2.1 %chunk.1 = (f32[8,160,128]{2,1,0:T(8,128)S(1)}, f32[6,128,128]{2,1,0:T(8,128)S(1)}) custom-call(bf16[4,128,128]{2,1,0:T(8,128)(2,1)S(1)} %pad_maximum_fusion.proj_ref, f32[3,128]{1,0:T(4,128)S(1)} %select_maximum_fusion.gate_rows_ref), custom_call_target="tpu_custom_call" | custom-call | tf_op jit(solution)/shard_map/chunk/pallas_call | solution.py:336
  3.7 25.5 %all_to_all.15.in_ref = f32[8,160,128]{2,1,0:T(8,128)S(1)} all-to-all(f32[8,160,128]{2,1,0:T(8,128)S(1)} %get-tuple-element.13), channel_id=1, replica_groups=mesh['x'=4,'y'=8,'z'=8,'c'=2] {'y'}, dimensions={0} | all-to-all | bytes 1310720 | tf_op jit(solution)/shard_map/all_to_all | solution.py:360
  29.3 1.1 %row.1 = (f32[32,32,128]{2,1,0:T(8,128)S(1)}, f32[2,128,128]{2,1,0:T(8,128)S(1)}) custom-call(f32[8,160,128]{2,1,0:T(8,128)S(1)} %all_to_all.15.in_ref), custom_call_target="tpu_custom_call" | custom-call | tf_op jit(solution)/shard_map/row/pallas_call | solution.py:336
  30.4 19.4 %all_to_all.16.in_ref = f32[32,32,128]{2,1,0:T(8,128)S(1)} all-to-all(f32[32,32,128]{2,1,0:T(8,128)S(1)} %get-tuple-element.15), channel_id=1, replica_groups={{112,240,368,496,96,224,352,480,80,208,336,464,64,192,320,448,48,176,30..., dimensions={0} | all-to-all | bytes 1048576 | tf_op jit(solution)/shard_map/all_to_all | solution.py:369
  49.8 0.0 copy-done
  49.8 0.0 copy-done.1
  49.8 1.8 %grad.1 = (f32[8,128,128]{2,1,0:T(8,128)S(1)}, bf16[3,128,128]{2,1,0:T(8,128)(2,1)S(1)}, f32[128,128]{1,0:T(8,128)S(1)}) custom-call(bf16[4,128,128]{2,1,0:T(8,128)(2,1)S(1)} %pad_maximum_fusion.proj_ref, f32[3,128]{1,0:T(4,128)S(1)} %select_maximum_fusion.gate_rows_ref, bf16[3,2048,128]{2,1,0:T(8,128)(2,1)S(1)} %copy-done, bf16[2,2048]{1,0:T(2,128)(2,1)S(1)} %bitcast.4, ...), custom_call_target="tpu_custom_call" | custom-call | tf_op jit(solution)/shard_map/grad/pallas_call | solution.py:336
  51.6 6.3 %collective-permute-start = (f32[8,128,128]{2,1,0:T(8,128)S(1)}, f32[8,128,128]{2,1,0:T(8,128)S(1)}, u32[]{:S(2)}, u32[]{:S(2)}) collective-permute-start(f32[8,128,128]{2,1,0:T(8,128)S(1)} %get-tuple-element.18), channel_id=1, source_target_pairs={{0,1},{1,0},{2,3},{3,2},{4,5},{5,4},{6,7},{7,6},{8,9},{9,8},{10,11... | collective-permute-start | bytes 1572872 | tf_op jit(solution)/shard_map/ppermute | solution.py:389
  58.0 0.5 keep.1
  58.5 1.0 %collective-permute-done = f32[8,128,128]{2,1,0:T(8,128)S(1)} collective-permute-done((f32[8,128,128]{2,1,0:T(8,128)S(1)}, f32[8,128,128]{2,1,0:T(8,128)S(1)}, u32[]{:S(2)}, u32[]{:S(2)}) %collective-permute-start) | collective-permute-done | bytes 524320 | tf_op jit(solution)/shard_map/ppermute | solution.py:389
  59.5 0.1 add.5
  59.6 23.0 %all_to_all.17 = f32[8,128,128]{2,1,0:T(8,128)S(1)} all-to-all(f32[8,128,128]{2,1,0:T(8,128)S(1)} %add.5), channel_id=1, replica_groups={{14,12,10,8,6,4,2,0},{15,13,11,9,7,5,3,1},{30,28,26,24,22,20,18,16},{31..., dimensions={0} | all-to-all | bytes 1048576 | tf_op jit(solution)/shard_map/all_to_all | solution.py:401
  82.6 0.6 reduce_sum.9
Async XLA Ops:
  1.6 48.2 %copy-start = (bf16[3,2048,128]{2,1,0:T(8,128)(2,1)S(1)}, bf16[3,2048,128]{2,1,0:T(8,128)(2,1)}, u32[]{:S(2)}) copy-start(bf16[3,2048,128]{2,1,0:T(8,128)(2,1)} %weight_ref.3) | copy-start | bytes 4718596
  1.6 48.2 %copy-start.1 = (bf16[2,1,2048]{2,0,1:T(2,128)(2,1)S(1)}, bf16[2,1,2048]{2,0,1:T(2,128)(2,1)}, u32[]{:S(2)}) copy-start(bf16[2,1,2048]{2,0,1:T(2,128)(2,1)} %param.11) | copy-start | bytes 24580
  51.6 7.9 %collective-permute-start = (f32[8,128,128]{2,1,0:T(8,128)S(1)}, f32[8,128,128]{2,1,0:T(8,128)S(1)}, u32[]{:S(2)}, u32[]{:S(2)}) collective-permute-start(f32[8,128,128]{2,1,0:T(8,128)S(1)} %get-tuple-element.18), channel_id=1, source_target_pairs={{0,1},{1,0},{2,3},{3,2},{4,5},{5,4},{6,7},{7,6},{8,9},{9,8},{10,11... | collective-permute-start | bytes 1572872 | tf_op jit(solution)/shard_map/ppermute | solution.py:389
